TPU v7x, 16 devices: a whole 2x2x2 slice. The times are simulated.
16 devices in a mesh: data: 4 (over z, y), model: 4 (over x, core).
Axes of the slice: x: 2, y: 2, z: 2, core: 2. Of those that a mesh axis runs over, the one named last changes fastest.
Arguments:
- hidden_in: bfloat16 [512, 3584], P('data'), parts along dimension 0
- positions: int32 [512], P('data'), parts along dimension 0
- norm_attn: bfloat16 [3, 3584], replicated
- norm_mlp: bfloat16 [3, 3584], replicated
- w_query: bfloat16 [3, 3584, 3584], P(None, None, 'model')
- w_key: bfloat16 [3, 3584, 512], P(None, None, 'model')
- w_value: bfloat16 [3, 3584, 512], P(None, None, 'model')
- w_out: bfloat16 [3, 3584, 3584], P(None, 'model')
- w_gate: bfloat16 [3, 3584, 18944], P(None, None, 'model')
- w_up: bfloat16 [3, 3584, 18944], P(None, None, 'model')
- w_down: bfloat16 [3, 18944, 3584], P(None, 'model')
- key_cache: bfloat16 [3, 512, 32, 4, 128], P(None, 'data', None, 'model'), parts along dimension 1
- value_cache: bfloat16 [3, 512, 32, 4, 128], P(None, 'data', None, 'model'), parts along dimension 1
Outputs:
- output 1: bfloat16 [512, 3584], P('data'), parts along dimension 0
- output 2: bfloat16 [3, 512, 32, 4, 128], P(None, 'data', None, 'model'), parts along dimension 1
- output 3: bfloat16 [3, 512, 32, 4, 128], P(None, 'data', None, 'model'), parts along dimension 1
There are 4 independent parts. A program takes and returns all parts, laid end to end along the dimension named above; an argument that names none is the same for every part.
All inputs are finite; a program needn't handle non-finite values.
Results may differ from a plain program's by a relative error of at most 0.02.
Values are sent between devices in bfloat16 or wider.
A program may use at most 1.5 GiB of HBM per device.

v0:
```python
import jax
import jax.numpy as jnp
from jax import lax
from jax.sharding import PartitionSpec as P

NORM_EPS = 1e-6
ROPE_BASE = 10000.0


def rms_norm(vals, gain):
    vals_f = vals.astype(jnp.float32)
    inv_rms = lax.rsqrt(jnp.mean(vals_f * vals_f, axis=-1, keepdims=True) + NORM_EPS)
    return (vals_f * inv_rms * gain.astype(jnp.float32)).astype(jnp.bfloat16)


def rope_tables(positions, head_dim):
    half = head_dim // 2
    inv_freq = ROPE_BASE ** (-jnp.arange(half, dtype=jnp.float32) / half)
    angles = positions.astype(jnp.float32)[:, None] * inv_freq[None, :]
    return jnp.cos(angles), jnp.sin(angles)


def apply_rope(vals, cos_tab, sin_tab):
    half = vals.shape[-1] // 2
    vals_f = vals.astype(jnp.float32)
    first = vals_f[..., :half]
    second = vals_f[..., half:]
    cos_b = cos_tab[:, None, :]
    sin_b = sin_tab[:, None, :]
    return jnp.concatenate([first * cos_b - second * sin_b, second * cos_b + first * sin_b], axis=-1).astype(jnp.bfloat16)


def attention(hidden, positions, cos_tab, sin_tab, q_proj, k_proj, v_proj, k_cache, v_cache):
    batch = hidden.shape[0]
    cache_len = k_cache.shape[1]
    kv_heads = k_cache.shape[2]
    head_dim = k_cache.shape[3]
    q_heads = q_proj.shape[1] // head_dim
    group = q_heads // kv_heads
    query = jnp.dot(hidden, q_proj, preferred_element_type=jnp.float32).astype(jnp.bfloat16).reshape(batch, q_heads, head_dim)
    key_new = jnp.dot(hidden, k_proj, preferred_element_type=jnp.float32).astype(jnp.bfloat16).reshape(batch, kv_heads, head_dim)
    value_new = jnp.dot(hidden, v_proj, preferred_element_type=jnp.float32).astype(jnp.bfloat16).reshape(batch, kv_heads, head_dim)
    query = apply_rope(query, cos_tab, sin_tab)
    key_new = apply_rope(key_new, cos_tab, sin_tab)
    slots = jnp.arange(cache_len)
    write_row = (slots[None, :] == positions[:, None])[:, :, None, None]
    k_cache = jnp.where(write_row, key_new[:, None], k_cache)
    v_cache = jnp.where(write_row, value_new[:, None], v_cache)
    query_g = query.reshape(batch, kv_heads, group, head_dim)
    scores = jnp.einsum("bkgd,bskd->bkgs", query_g, k_cache, preferred_element_type=jnp.float32) * (head_dim ** -0.5)
    visible = (slots[None, :] <= positions[:, None])[:, None, None, :]
    scores = jnp.where(visible, scores, -1e30)
    attn_prob = jax.nn.softmax(scores, axis=-1).astype(jnp.bfloat16)
    attn_val = jnp.einsum("bkgs,bskd->bkgd", attn_prob, v_cache, preferred_element_type=jnp.float32).astype(jnp.bfloat16)
    return attn_val.reshape(batch, q_heads * head_dim), k_cache, v_cache


def gated_mlp(hidden, gate_proj, up_proj):
    gate_pre = jnp.dot(hidden, gate_proj, preferred_element_type=jnp.float32)
    up_val = jnp.dot(hidden, up_proj, preferred_element_type=jnp.float32)
    return (jax.nn.silu(gate_pre) * up_val).astype(jnp.bfloat16)


def add_residual(residual, delta):
    return (residual.astype(jnp.float32) + delta.astype(jnp.float32)).astype(jnp.bfloat16)


def solution(mesh):
    def local_step(hidden_in, positions, norm_attn, norm_mlp, w_query, w_key, w_value, w_out, w_gate, w_up, w_down, key_cache, value_cache):
        cos_tab, sin_tab = rope_tables(positions, key_cache.shape[-1])
        residual = hidden_in
        key_list = []
        value_list = []
        for layer in range(key_cache.shape[0]):
            hidden = rms_norm(residual, norm_attn[layer])
            attn_val, kc_new, vc_new = attention(hidden, positions, cos_tab, sin_tab, w_query[layer], w_key[layer], w_value[layer], key_cache[layer], value_cache[layer])
            key_list.append(kc_new)
            value_list.append(vc_new)
            attn_part = jnp.dot(attn_val, w_out[layer], preferred_element_type=jnp.float32).astype(jnp.bfloat16)
            residual = add_residual(residual, lax.psum(attn_part, "model"))
            hidden = rms_norm(residual, norm_mlp[layer])
            act_val = gated_mlp(hidden, w_gate[layer], w_up[layer])
            mlp_part = jnp.dot(act_val, w_down[layer], preferred_element_type=jnp.float32).astype(jnp.bfloat16)
            residual = add_residual(residual, lax.psum(mlp_part, "model"))
        return residual, jnp.stack(key_list), jnp.stack(value_list)

    row_spec = P("data", None)
    col_spec = P(None, None, "model")
    split_spec = P(None, "model", None)
    cache_spec = P(None, "data", None, "model", None)
    in_specs = (row_spec, P("data"), P(None, None), P(None, None), col_spec, col_spec, col_spec, split_spec, col_spec, col_spec, split_spec, cache_spec, cache_spec)
    out_specs = (row_spec, cache_spec, cache_spec)
    return jax.shard_map(local_step, mesh=mesh, in_specs=in_specs, out_specs=out_specs, check_vma=False)
```

profile of v0, /device:TPU:0, one launch (start us, length us, event | category | flops | bytes accessed | tf_op | source)
XLA Modules:
  0.0 407.6 jit_solution(8575650710772472168)
XLA Ops:
  7.2 0.7 convert_element_type.242
  8.0 0.7 iota_compare_fusion.1
  8.7 1.4 fusion.105
  10.2 1.0 convert_reduce_fusion.5
  11.2 1.9 convolution_convert_fusion.7
  13.1 1.7 fusion.160
  15.5 4.0 fusion.144
  20.4 3.6 fusion.261
  24.0 2.1 convolution_convert_fusion.2
  26.3 4.9 %fusion.66 = bf16[128,3584]{1,0:T(8,128)(2,1)} fusion(bf16[128,896]{0,1:T(8,128)(2,1)S(1)} %bitcast.194, bf16[3,896,3584]{2,1,0:T(8,128)(2,1)} %param.20), kind=kOutput, calls=%fused_computation.54 | convolution fusion | flops 822542336 | bytes 7569408 | tf_op jit(solution)/shard_map/dot_general | solution.py:79
  31.5 0.7 convert_reduce_fusion
  32.2 34.0 %all-reduce.7.cloned.1.call-done = bf16[128,3584]{1,0:T(8,128)(2,1)} async-done(((bf16[128,3584]{1,0:T(8,128)(2,1)}), bf16[128,3584]{1,0:T(8,128)(2,1)}) %all-reduce.7.cloned.1.call-update) | async-done | bytes 917520 | tf_op jit(solution)/shard_map/psum | solution.py:80
  66.2 1.6 fusion.109
  67.8 14.7 %fusion.19 = f32[128,4736]{1,0:T(8,128)} fusion(bf16[3,3584,4736]{2,1,0:T(8,128)(2,1)} %param.21, bf16[128,3584]{1,0:T(8,128)(2,1)S(1)} %get-tuple-element.20, f32[3584]{0:T(1024)S(1)} %get-tuple-element.10, f32[128]{0:T(128)S(1)} %add_rsqrt_fusion.4), kind=kOutput, calls=%fused_computation.19 | convolution fusion | flops 4347133952 | bytes 37304832 | tf_op jit(solution)/shard_map/dot_general | solution.py:59
  82.5 25.3 %fusion.75 = bf16[128,3584]{1,0:T(8,128)(2,1)} fusion(bf16[3,4736,3584]{2,1,0:T(8,128)(2,1)} %param.23, bf16[3,3584,4736]{2,1,0:T(8,128)(2,1)} %param.22, f32[128,4736]{1,0:T(8,128)} %fusion.19, bf16[128,3584]{1,0:T(8,128)(2,1)S(1)} %get-tuple-element.20, f32[3584]{0:T(1024)S(1)} %get-tuple-element.10, f32[128]{0:T(128)S(1)} %add_rsqrt_fusion.4), kind=kOutput, calls=%fused_computation.57 | convolution fusion | flops 8696528896 | bytes 72169984 | tf_op jit(solution)/shard_map/dot_general | solution.py:83
  107.9 32.0 %all-reduce.9.cloned.1.call-done = bf16[128,3584]{1,0:T(8,128)(2,1)} async-done(((bf16[128,3584]{1,0:T(8,128)(2,1)}), bf16[128,3584]{1,0:T(8,128)(2,1)}) %all-reduce.9.cloned.1.call-update) | async-done | bytes 917520 | tf_op jit(solution)/shard_map/psum | solution.py:84
  139.9 1.6 fusion.113
  141.6 0.3 fusion.115
  141.9 2.2 convolution_convert_fusion.5
  144.1 1.7 fusion.162
  145.8 4.0 fusion.150
  150.9 0.8 subtract_convert_fusion.1
  151.7 3.7 fusion.262
  155.4 2.1 convolution_convert_fusion.1
  157.7 4.9 %fusion.69 = bf16[128,3584]{1,0:T(8,128)(2,1)} fusion(bf16[128,896]{0,1:T(8,128)(2,1)S(1)} %bitcast.195, bf16[3,896,3584]{2,1,0:T(8,128)(2,1)} %param.20), kind=kOutput, calls=%fused_computation.55 | convolution fusion | flops 822542336 | bytes 7569408 | tf_op jit(solution)/shard_map/dot_general | solution.py:79
  162.9 31.9 %all-reduce.11.cloned.1.call-done = bf16[128,3584]{1,0:T(8,128)(2,1)} async-done(((bf16[128,3584]{1,0:T(8,128)(2,1)}), bf16[128,3584]{1,0:T(8,128)(2,1)}) %all-reduce.11.cloned.1.call-update) | async-done | bytes 917520 | tf_op jit(solution)/shard_map/psum | solution.py:80
  194.8 1.7 fusion.117
  196.5 14.7 %fusion.13 = f32[128,4736]{1,0:T(8,128)} fusion(bf16[3,3584,4736]{2,1,0:T(8,128)(2,1)} %param.21, bf16[128,3584]{1,0:T(8,128)(2,1)S(1)} %get-tuple-element.18, f32[3584]{0:T(1024)S(1)} %copy-done.12, f32[128]{0:T(128)S(1)} %add_rsqrt_fusion.2), kind=kOutput, calls=%fused_computation.13 | convolution fusion | flops 4347133952 | bytes 37304832 | tf_op jit(solution)/shard_map/dot_general | solution.py:59
  211.2 25.3 %fusion.78 = bf16[128,3584]{1,0:T(8,128)(2,1)} fusion(bf16[3,4736,3584]{2,1,0:T(8,128)(2,1)} %param.23, bf16[3,3584,4736]{2,1,0:T(8,128)(2,1)} %param.22, f32[128,4736]{1,0:T(8,128)} %fusion.13, bf16[128,3584]{1,0:T(8,128)(2,1)S(1)} %get-tuple-element.18, f32[3584]{0:T(1024)S(1)} %copy-done.12, f32[128]{0:T(128)S(1)} %add_rsqrt_fusion.2), kind=kOutput, calls=%fused_computation.58 | convolution fusion | flops 8696528896 | bytes 72169984 | tf_op jit(solution)/shard_map/dot_general | solution.py:83
  236.6 32.0 %all-reduce.13.cloned.1.call-done = bf16[128,3584]{1,0:T(8,128)(2,1)} async-done(((bf16[128,3584]{1,0:T(8,128)(2,1)}), bf16[128,3584]{1,0:T(8,128)(2,1)}) %all-reduce.13.cloned.1.call-update) | async-done | bytes 917520 | tf_op jit(solution)/shard_map/psum | solution.py:84
  268.7 1.6 fusion.121
  270.7 1.6 convolution_convert_fusion.3
  272.3 1.7 fusion.164
  274.0 4.0 fusion.156
  279.0 0.8 subtract_convert_fusion
  279.9 3.7 fusion.263
  283.5 2.1 convolution_convert_fusion
  285.9 4.9 %fusion.72 = bf16[128,3584]{1,0:T(8,128)(2,1)} fusion(bf16[128,896]{0,1:T(8,128)(2,1)S(1)} %bitcast.196, bf16[3,896,3584]{2,1,0:T(8,128)(2,1)} %param.20), kind=kOutput, calls=%fused_computation.56 | convolution fusion | flops 822542336 | bytes 7569408 | tf_op jit(solution)/shard_map/dot_general | solution.py:79
  291.1 5.8 %select_bitcast_fusion.1 = (bf16[1,128,32,1,128]{4,2,3,1,0:T(8,128)(2,1)}, bf16[1,128,32,1,128]{4,2,3,1,0:T(8,128)(2,1)}, bf16[1,128,32,1,128]{4,2,1,3,0:T(8,128...) fusion(pred[128,32]{1,0:T(8,128)(4,1)S(1)} %get-tuple-element.50, ...), kind=kLoop, calls=%fused_computation.163 | loop fusion | flops 2621440 | bytes 10653696 | tf_op jit(solution)/shard_map/jit(_where)/select_n | solution.py:48
  296.9 26.0 %all-reduce.15.cloned.1.call-done = bf16[128,3584]{1,0:T(8,128)(2,1)} async-done(((bf16[128,3584]{1,0:T(8,128)(2,1)}), bf16[128,3584]{1,0:T(8,128)(2,1)}) %all-reduce.15.cloned.1.call-update) | async-done | bytes 917520 | tf_op jit(solution)/shard_map/psum | solution.py:80
  322.9 2.5 fusion.125
  325.5 15.1 %fusion.7 = f32[128,4736]{1,0:T(8,128)} fusion(bf16[3,3584,4736]{2,1,0:T(8,128)(2,1)} %param.21, bf16[128,3584]{1,0:T(8,128)(2,1)} %get-tuple-element.16, f32[3584]{0:T(1024)S(1)} %copy-done.11, f32[128]{0:T(128)S(1)} %add_rsqrt_fusion), kind=kOutput, calls=%fused_computation.7 | convolution fusion | flops 4347133952 | bytes 37304832 | tf_op jit(solution)/shard_map/dot_general | solution.py:59
  340.6 25.3 %fusion.81 = bf16[128,3584]{1,0:T(8,128)(2,1)} fusion(bf16[3,4736,3584]{2,1,0:T(8,128)(2,1)} %param.23, bf16[3,3584,4736]{2,1,0:T(8,128)(2,1)} %param.22, f32[128,4736]{1,0:T(8,128)} %fusion.7, bf16[128,3584]{1,0:T(8,128)(2,1)S(1)} %copy-done.6, f32[3584]{0:T(1024)S(1)} %copy-done.11, f32[128]{0:T(128)S(1)} %add_rsqrt_fusion), kind=kOutput, calls=%fused_computation.59 | convolution fusion | flops 8696528896 | bytes 72169984 | tf_op jit(solution)/shard_map/dot_general | solution.py:83
  365.9 2.6 bitcast_select_fusion
  368.5 3.4 pad_maximum_fusion
  371.9 2.0 maximum_bitcast_fusion
  373.9 24.1 %all-reduce.17.cloned.1.call-done = bf16[128,3584]{1,0:T(8,128)(2,1)} async-done(((bf16[128,3584]{1,0:T(8,128)(2,1)}), bf16[128,3584]{1,0:T(8,128)(2,1)}) %all-reduce.17.cloned.1.call-update) | async-done | bytes 917520 | tf_op jit(solution)/shard_map/psum | solution.py:84
  398.0 2.3 fusion.128
  (80 shorter events, 5.6 us)
Async XLA Ops:
  7.2 5.9 %copy-start.5 = (bf16[128,3584]{1,0:T(8,128)(2,1)S(1)}, bf16[128,3584]{1,0:T(8,128)(2,1)}, u32[]{:S(2)}) copy-start(bf16[128,3584]{1,0:T(8,128)(2,1)} %param.13) | copy-start | bytes 2752516
  7.2 59.0 %all-reduce.7.cloned.1.call-start = ((), (), s32[]{:S(2)}) async-start(), calls=%async_computation | async-start | bytes 1835008 | tf_op jit(solution)/shard_map/psum | solution.py:80
  7.2 142.6 %copy-start.13 = (f32[64]{0:T(128)}, f32[64]{0:T(128)S(1)}, u32[]{:S(2)}) copy-start(f32[64]{0:T(128)S(1)} %multiply_power_fusion) | copy-start | bytes 772
  8.0 141.8 %copy-start.15 = (f32[128]{0:T(128)}, f32[128]{0:T(128)S(1)}, u32[]{:S(2)}) copy-start(f32[128]{0:T(128)S(1)} %convert_element_type.242) | copy-start | bytes 1540
  26.3 5.2 %copy-start.8 = (bf16[3,3584]{1,0:T(4,128)(2,1)S(1)}, bf16[3,3584]{1,0:T(4,128)(2,1)}, u32[]{:S(2)}) copy-start(bf16[3,3584]{1,0:T(4,128)(2,1)} %param.16) | copy-start | bytes 64516
  31.2 108.7 %all-reduce.9.cloned.1.call-start = ((), (), s32[]{:S(2)}) async-start(), calls=%async_computation.1 | async-start | bytes 1835008 | tf_op jit(solution)/shard_map/psum | solution.py:84
  107.8 87.0 %all-reduce.11.cloned.1.call-start = ((), (), s32[]{:S(2)}) async-start(), calls=%async_computation.2 | async-start | bytes 1835008 | tf_op jit(solution)/shard_map/psum | solution.py:80
  139.9 1.6 copy-start.1
  150.9 4.5 %copy-start.9 = (bf16[128,128]{1,0:T(8,128)(2,1)S(1)}, bf16[128,128]{1,0:T(8,128)(2,1)}, u32[]{:S(2)}) copy-start(bf16[128,128]{1,0:T(8,128)(2,1)} %convolution_convert_fusion.5) | copy-start | bytes 98308
  162.6 33.9 %copy-start.12 = (f32[3584]{0:T(1024)S(1)}, f32[3584]{0:T(1024)}, u32[]{:S(2)}) copy-start(f32[3584]{0:T(1024)} %get-tuple-element.11) | copy-start | bytes 43012
  162.7 106.0 %all-reduce.13.cloned.1.call-start = ((), (), s32[]{:S(2)}) async-start(), calls=%async_computation.3 | async-start | bytes 1835008 | tf_op jit(solution)/shard_map/psum | solution.py:84
  236.6 86.4 %all-reduce.15.cloned.1.call-start = ((), (), s32[]{:S(2)}) async-start(), calls=%async_computation.4 | async-start | bytes 1835008 | tf_op jit(solution)/shard_map/psum | solution.py:80
  268.7 1.6 copy-start
  273.9 4.0 copy-start.14
  274.0 4.0 copy-start.16
  285.9 5.2 %copy-start.10 = (bf16[128,128]{1,0:T(8,128)(2,1)S(1)}, bf16[128,128]{1,0:T(8,128)(2,1)}, u32[]{:S(2)}) copy-start(bf16[128,128]{1,0:T(8,128)(2,1)} %convolution_convert_fusion.5) | copy-start | bytes 98308
  290.8 107.2 %all-reduce.17.cloned.1.call-start = ((), (), s32[]{:S(2)}) async-start(), calls=%async_computation.5 | async-start | bytes 1835008 | tf_op jit(solution)/shard_map/psum | solution.py:84
  296.9 28.6 %copy-start.11 = (f32[3584]{0:T(1024)S(1)}, f32[3584]{0:T(1024)}, u32[]{:S(2)}) copy-start(f32[3584]{0:T(1024)} %get-tuple-element.9) | copy-start | bytes 43012
  325.5 15.1 %copy-start.6 = (bf16[128,3584]{1,0:T(8,128)(2,1)S(1)}, bf16[128,3584]{1,0:T(8,128)(2,1)}, u32[]{:S(2)}) copy-start(bf16[128,3584]{1,0:T(8,128)(2,1)} %get-tuple-element.16) | copy-start | bytes 2752516
  365.9 2.6 copy-start.4
  368.5 3.4 copy-start.2
  368.5 3.4 copy-start.3
  371.9 26.1 %copy-start.7 = (bf16[128,3584]{1,0:T(8,128)(2,1)S(1)}, bf16[128,3584]{1,0:T(8,128)(2,1)}, u32[]{:S(2)}) copy-start(bf16[128,3584]{1,0:T(8,128)(2,1)} %get-tuple-element.16) | copy-start | bytes 2752516
Sparse Core Ops, SparseCore 0:
  31.3 34.7 all-reduce.6
  107.9 31.9 all-reduce.8
  162.8 31.9 all-reduce.10
  236.7 31.9 all-reduce.12
  290.9 31.9 all-reduce.14
  366.0 31.9 all-reduce.16
where the time goes:
time: 413 us; the launch traced here: 408 us
  waiting for transfers between devices  180 us (44%)
  matrix products  175 us (42%)
  other arithmetic  33.3 us (8%)
  between operations  15.1 us (4%)
    psum x3, waiting for transfers between devices, local_step(): residual = add_residual(residual, lax.psum(attn_part, 'model'))  91.9 us
    psum x3, waiting for transfers between devices, local_step(): residual = add_residual(residual, lax.psum(mlp_part, 'model'))  88.2 us
    dot_general x3, matrix products, local_step(): jnp.dot(act_val, w_down[layer], preferred_element_type=jnp.float32)  75.9 us
    dot_general x3, matrix products, gated_mlp(): gate_pre = jnp.dot(hidden, gate_proj, preferred_element_type=jnp.float32)  44.5 us
    dot_general x3, matrix products, local_step(): jnp.dot(attn_val, w_out[layer], preferred_element_type=jnp.float32)  14.7 us
    dot_general x3, matrix products, attention(): jnp.dot(hidden, q_proj, preferred_element_type=jnp.float32)  12 us
    sub x3, matrix products, attention(): attn_prob = jax.nn.softmax(scores, axis=-1).astype(jnp.bfloat16)  10.9 us
    reduce_sum x6, other arithmetic, rms_norm(): jnp.mean(vals_f * vals_f, axis=-1, keepdims=True) + NORM_EPS  10.5 us
  transfers between devices with their start and end apart: 6, of which 6 were waited for; matrix products, arithmetic and copies ran while one was open for 4% of the time, Pallas kernels for 0%

commit v1 on v0

v1 whole, which is shorter than its diff:
```python
import functools

import jax
import jax.numpy as jnp
import numpy as np
from jax import lax
from jax.experimental import pallas as pl
from jax.experimental.pallas import tpu as pltpu
from jax.sharding import PartitionSpec as P

NORM_EPS = 1e-6
ROPE_BASE = 10000.0
MESH = pl.DeviceIdType.MESH
F32 = jnp.float32
BF16 = jnp.bfloat16

LAYERS = 3
ROWS = 128
DIM = 3584
HD = 128
QH = 7
CACHE = 32
FF = 4736
BLKS = DIM // 128
CH = DIM // 256
PAIRS = DIM // 512
QKV = (QH + 2) * HD
PER_LAYER = 4 + 4 + 4 * PAIRS + CH
TOTAL = LAYERS * PER_LAYER
SLOTS = 17
DOWN = 2.0 ** -32
UP = 2.0 ** 32
GROUP = 8
UNROLL = 8


def kernel(x_hbm, pos_ref, na_ref, nm_ref, freq_ref, wq, wk, wv, wo, wg, wu, wd, kc_hbm, vc_hbm,
           out_hbm, kn_out, vn_out,
           ring, ring_sem, x, x_sem, gn, posb, cos_t, sin_t, vis, ss, qkv, qs, kn, vn, at, ab, acc_g, acc_u, act,
           kbuf, vbuf, kv_sem, own, a_send, a_recv, b_send, b_recv, a_ss, a_rs, b_ss, b_rs, c_ss, c_rs):
    me = lax.axis_index("model")
    core = lax.rem(me, 2)
    partner = me + 1 - 2 * core
    peer = lax.rem(me + 2, 4)

    def slot_of(n):
        return lax.rem(n, SLOTS)

    def issue(n):
        layer = n // PER_LAYER
        r = n - layer * PER_LAYER
        s = slot_of(n)
        live = n < TOTAL

        def copy(src, dst):
            pltpu.make_async_copy(src, dst, ring_sem.at[s]).start()

        def qkv_part(r, parts):
            for t in range(parts):
                rows = pl.ds(pl.multiple_of((r * 4 + t) * 256, 256), 256)
                base = t * QKV
                copy(wq.at[layer, rows, :], ring.at[s, :, base:base + QH * HD])
                copy(wk.at[layer, rows, :], ring.at[s, :, base + QH * HD:base + (QH + 1) * HD])
                copy(wv.at[layer, rows, :], ring.at[s, :, base + (QH + 1) * HD:base + QKV])

        @pl.when(live & (r < 3))
        def _():
            qkv_part(r, 4)

        @pl.when(live & (r == 3))
        def _():
            qkv_part(3, 2)

        @pl.when(live & (r >= 4) & (r < 7))
        def _():
            copy(wo.at[layer, pl.ds(pl.multiple_of((r - 4) * 256, 256), 256), :], ring.at[s, :, :DIM])

        @pl.when(live & (r == 7))
        def _():
            copy(wo.at[layer, 768:896, :], ring.at[s, :128, :DIM])

        gu = r - 8
        row0 = 512 * (gu // 4) + 256 * lax.rem(gu, 2)

        @pl.when(live & (r >= 8) & (r < 36) & (lax.rem(gu, 4) < 2))
        def _():
            copy(wg.at[layer, pl.ds(pl.multiple_of(row0, 256), 256), :], ring.at[s])

        @pl.when(live & (r >= 8) & (r < 36) & (lax.rem(gu, 4) >= 2))
        def _():
            copy(wu.at[layer, pl.ds(pl.multiple_of(row0, 256), 256), :], ring.at[s])

        @pl.when(live & (r >= 36))
        def _():
            cols = pl.ds(pl.multiple_of((r - 36) * 256, 256), 256)
            for b in range(18):
                copy(wd.at[layer, b * 256:b * 256 + 256, cols], ring.at[s, :, b * 256:b * 256 + 256])
            c0 = pl.ds(pl.multiple_of((r - 36) * 256, 128), 128)
            c1 = pl.ds(pl.multiple_of((r - 36) * 256 + 128, 128), 128)
            copy(wd.at[layer, 4608:4736, c0], ring.at[s, :128, 4608:4736])
            copy(wd.at[layer, 4608:4736, c1], ring.at[s, 128:, 4608:4736])

    def wait_slot(n, rows, cols):
        s = slot_of(n)
        pltpu.make_async_copy(wg.at[0, :rows, :cols], ring.at[s, :rows, :cols], ring_sem.at[s]).wait()

    def kv_copies(layer):
        b = lax.rem(layer, 2)
        return (pltpu.make_async_copy(kc_hbm.at[layer], kbuf.at[b], kv_sem.at[0, b]),
                pltpu.make_async_copy(vc_hbm.at[layer], vbuf.at[b], kv_sem.at[1, b]))

    barrier = pltpu.get_barrier_semaphore()
    for other in (partner, peer):
        pl.semaphore_signal(barrier, inc=1, device_id={"model": other}, device_id_type=MESH)

    def load_x(b, carry):
        pltpu.make_async_copy(x_hbm.at[:, pl.ds(pl.multiple_of(b * 128, 128), 128)], x.at[b], x_sem).start()
        return carry

    lax.fori_loop(0, BLKS, load_x, 0)

    def prologue(n, carry):
        issue(n)
        return carry

    lax.fori_loop(0, 4, prologue, 0)
    for cp in kv_copies(0):
        cp.start()
    lax.fori_loop(4, SLOTS, prologue, 0)

    for layer in range(LAYERS):
        for which, ref in enumerate((na_ref, nm_ref)):
            row = ref[layer:layer + 1, :].astype(F32) * DOWN
            gn[2 * layer + which] = jnp.broadcast_to(row, (8, DIM))
    pos_row = jnp.broadcast_to(pos_ref[...].astype(F32), (ROWS, ROWS))
    ri = lax.broadcasted_iota(jnp.int32, (ROWS, ROWS), 0)
    ci = lax.broadcasted_iota(jnp.int32, (ROWS, ROWS), 1)
    pos_col = jnp.sum(jnp.where(ri == ci, pos_row, 0.0), axis=1, keepdims=True)
    pos_b = jnp.broadcast_to(pos_col, (ROWS, HD))
    posb[...] = pos_b
    angle = pos_b * freq_ref[...]
    cos_t[...] = jnp.cos(angle)
    sin_v = jnp.sin(angle)
    sin_t[...] = jnp.where(ci < HD // 2, -sin_v, sin_v)
    r2 = lax.broadcasted_iota(jnp.int32, (ROWS, GROUP * CACHE), 0)
    c2 = lax.broadcasted_iota(jnp.int32, (ROWS, GROUP * CACHE), 1)
    mine = (c2 // CACHE) == lax.rem(r2, GROUP)
    seen = lax.rem(c2, CACHE).astype(F32) <= jnp.broadcast_to(pos_col, (ROWS, GROUP * CACHE))
    vis[...] = jnp.where(mine & seen, 1.0, 0.0)

    pltpu.make_async_copy(x, x, x_sem).wait()
    pl.semaphore_wait(barrier, 2)

    def a_copy(j):
        return pltpu.make_async_remote_copy(a_send.at[j], a_recv.at[j], a_ss.at[j], a_rs.at[j],
                                            device_id={"model": partner}, device_id_type=MESH)

    def b_copy(p, j):
        return pltpu.make_async_remote_copy(b_send.at[j], b_recv.at[p, j], b_ss.at[j], b_rs.at[p, j],
                                            device_id={"model": peer}, device_id_type=MESH)

    def c_copy(j, half):
        blk = 2 * j + half
        return pltpu.make_async_remote_copy(x.at[blk], x.at[blk], c_ss.at[j], c_rs.at[j],
                                            device_id={"model": partner}, device_id_type=MESH)

    def stage_a(j, part):
        lo, hi = part[:, :128], part[:, 128:]
        first = core == 0
        own[j] = jnp.where(first, lo, hi)
        a_send[j] = jnp.where(first, hi, lo).astype(BF16)
        a_copy(j).start()

    def stage_b(p, j):
        a_copy(j).wait_recv()
        b_send[j] = (own[j] + a_recv[j].astype(F32)).astype(BF16)
        b_copy(p, j).start()

    def stage_c(p, j):
        b_copy(p, j).wait_recv()
        total = b_send[j].astype(F32) + b_recv[p, j].astype(F32)
        blk = 2 * j + core
        x[blk] = (x[blk].astype(F32) + total).astype(BF16)
        c_copy(j, core).start()
        a_copy(j).wait_send()
        b_copy(p, j).wait_send()

    def stage_d(j):
        c_copy(j, 1 - core).wait_recv()
        c_copy(j, core).wait_send()

    def stage_c2(p, i):
        stage_c(p, 2 * i)
        stage_c(p, 2 * i + 1)

    def stage_d2(i):
        stage_d(2 * i)
        stage_d(2 * i + 1)

    def take(row, i):
        outs = []
        sq = ss[...]
        for b in range(4):
            blk = x[4 * i + b].astype(F32)
            sq = sq + blk * blk
            gain = gn[row, 0:1, pl.ds(pl.multiple_of(i * 512 + b * 128, 128), 128)]
            outs.append((blk * gain).astype(BF16))
        ss[...] = sq
        return (jnp.concatenate(outs[:2], axis=1), jnp.concatenate(outs[2:], axis=1))

    def row_scale():
        mean = jnp.sum(ss[...], axis=1, keepdims=True) * (1.0 / DIM)
        return lax.rsqrt(mean + NORM_EPS) * UP

    def dot(a, b):
        return jnp.dot(a, b, preferred_element_type=F32)

    def tiles(width, step):
        return [(n, min(step, width - n)) for n in range(0, width, step)]

    def layer_body(layer, carry):
        base = layer * PER_LAYER
        ss[...] = jnp.zeros_like(ss)
        qkv[...] = jnp.zeros_like(qkv)

        @pl.when(layer > 0)
        def _():
            stage_c2(1, 0)

        def qkv_step(i, carry):
            @pl.when((layer > 0) & (i + 1 < PAIRS))
            def _():
                stage_c2(1, i + 1)

            @pl.when(layer > 0)
            def _():
                stage_d2(i)

            n = base + i // 2
            half = lax.rem(i, 2)

            @pl.when((half == 0) & (i < 6))
            def _():
                wait_slot(n, 256, 4 * QKV)

            @pl.when(i == 6)
            def _():
                wait_slot(n, 256, 2 * QKV)

            h0, h1 = take(2 * layer, i)
            s = slot_of(n)
            for c0, w in tiles(QKV, 512):
                o0 = pl.ds(pl.multiple_of(half * 2 * QKV + c0, 128), w)
                o1 = pl.ds(pl.multiple_of(half * 2 * QKV + QKV + c0, 128), w)
                qkv[:, c0:c0 + w] += dot(h0, ring[s, :, o0]) + dot(h1, ring[s, :, o1])

            @pl.when((half == 1) | (i == 6))
            def _():
                issue(n + SLOTS)

            return carry

        lax.fori_loop(0, PAIRS, qkv_step, 0)

        scale = row_scale()
        cos_v, sin_v = cos_t[...], sin_t[...]

        def head(idx):
            return (qkv[:, idx * HD:(idx + 1) * HD] * scale).astype(BF16)

        def rotate(v):
            v = v.astype(F32)
            return (v * cos_v + pltpu.roll(v, HD // 2, axis=1) * sin_v).astype(BF16)

        for h in range(QH):
            qs[h] = rotate(head(h)).astype(F32)
        k_new = rotate(head(QH))
        v_new = head(QH + 1)
        kn[...] = k_new.astype(F32)
        vn[...] = v_new.astype(F32)
        kn_out[layer] = k_new
        vn_out[layer] = v_new
        for cp in kv_copies(layer):
            cp.wait()
        buf = lax.rem(layer, 2)
        srow = lax.rem(lax.broadcasted_iota(jnp.int32, (GROUP * CACHE, HD), 0), CACHE).astype(F32)

        def spread(v):
            return jnp.broadcast_to(v[:, None, :], (GROUP, CACHE, HD)).reshape(GROUP * CACHE, HD)

        def attend(g):
            rows = pl.ds(pl.multiple_of(g * GROUP, GROUP), GROUP)
            crow = pl.ds(pl.multiple_of(g * GROUP * CACHE, GROUP * CACHE), GROUP * CACHE)
            q = jnp.concatenate([qs[h, rows, :] for h in range(QH)] + [qs[0, rows, :]], axis=0).astype(BF16)
            here = srow == spread(posb[rows, :])
            keys = jnp.where(here, spread(kn[rows, :]), kbuf[buf, crow, :].astype(F32)).astype(BF16)
            vals = jnp.where(here, spread(vn[rows, :]), vbuf[buf, crow, :].astype(F32)).astype(BF16)
            sc = lax.dot_general(q, keys, (((1,), (1,)), ((), ())), preferred_element_type=F32)
            sc = (sc * (HD ** -0.5)).reshape(QH + 1, GROUP, GROUP * CACHE)
            ok = (vis[rows, :] > 0.5)[None]
            sc = jnp.where(ok, sc, -1e30)
            e = jnp.exp(sc - jnp.max(sc, axis=-1, keepdims=True))
            prob = e * (1.0 / jnp.sum(e, axis=-1, keepdims=True))
            o = dot(prob.reshape((QH + 1) * GROUP, GROUP * CACHE).astype(BF16), vals)
            for h in range(QH):
                at[h, rows, :] = o[h * GROUP:(h + 1) * GROUP]

        def attend_some(gg, carry):
            for u in range(UNROLL):
                attend(gg * UNROLL + u)
            return carry

        lax.fori_loop(0, ROWS // GROUP // UNROLL, attend_some, 0)

        @pl.when(layer + 1 < LAYERS)
        def _():
            for cp in kv_copies(layer + 1):
                cp.start()

        for h in range(QH):
            ab[:, h * HD:(h + 1) * HD] = at[h].astype(BF16)

        for b in range(3):
            wait_slot(base + 4 + b, 256, DIM)
        wait_slot(base + 7, 128, DIM)

        def out_step(j, carry):
            cols = pl.ds(pl.multiple_of(j * 256, 256), 256)
            part = dot(ab[:, 768:896], ring[slot_of(base + 7), :128, cols])
            for b in range(3):
                part = part + dot(ab[:, b * 256:(b + 1) * 256], ring[slot_of(base + 4 + b), :, cols])
            stage_a(j, part)

            @pl.when(j >= 2)
            def _():
                stage_b(0, j - 2)

            return carry

        lax.fori_loop(0, CH, out_step, 0)
        for b in range(4):
            issue(base + 4 + b + SLOTS)
        stage_b(0, CH - 2)
        stage_b(0, CH - 1)

        ss[...] = jnp.zeros_like(ss)
        acc_g[...] = jnp.zeros_like(acc_g)
        acc_u[...] = jnp.zeros_like(acc_u)
        stage_c2(0, 0)

        def gu_step(i, carry):
            @pl.when(i + 1 < PAIRS)
            def _():
                stage_c2(0, i + 1)

            stage_d2(i)
            h0, h1 = take(2 * layer + 1, i)
            n = base + 8 + 4 * i
            for k, acc in ((0, acc_g), (2, acc_u)):
                wait_slot(n + k, 256, FF)
                wait_slot(n + k + 1, 256, FF)
                s0, s1 = slot_of(n + k), slot_of(n + k + 1)
                for c0, w in tiles(FF, 512):
                    acc[:, c0:c0 + w] += dot(h0, ring[s0, :, c0:c0 + w]) + dot(h1, ring[s1, :, c0:c0 + w])
                issue(n + k + SLOTS)
                issue(n + k + 1 + SLOTS)
            return carry

        lax.fori_loop(0, PAIRS, gu_step, 0)
        scale2 = row_scale()
        for c0, w in tiles(FF, 512):
            gate = acc_g[:, c0:c0 + w] * scale2
            up = acc_u[:, c0:c0 + w] * scale2
            act[:, c0:c0 + w] = (gate * jax.nn.sigmoid(gate) * up).astype(BF16)

        def down_step(j, carry):
            n = base + 36 + j
            s = slot_of(n)
            wait_slot(n, 256, FF)
            parts = [jnp.zeros((ROWS, 256), F32), jnp.zeros((ROWS, 256), F32)]
            for b in range(18):
                parts[b % 2] = parts[b % 2] + dot(act[:, b * 256:(b + 1) * 256], ring[s, :, b * 256:(b + 1) * 256])
            last = jnp.concatenate([ring[s, :128, 4608:4736], ring[s, 128:, 4608:4736]], axis=1)
            part = parts[0] + (parts[1] + dot(act[:, 4608:4736], last))
            stage_a(j, part)
            issue(n + SLOTS)

            @pl.when(j >= 2)
            def _():
                stage_b(1, j - 2)

            return carry

        lax.fori_loop(0, CH, down_step, 0)
        stage_b(1, CH - 2)
        stage_b(1, CH - 1)
        return carry

    lax.fori_loop(0, LAYERS, layer_body, 0)

    stage_c2(1, 0)

    def last_step(i, carry):
        @pl.when(i + 1 < PAIRS)
        def _():
            stage_c2(1, i + 1)

        stage_d2(i)
        for b in range(4):
            blk = 4 * i + b
            pltpu.make_async_copy(x.at[blk], out_hbm.at[:, pl.ds(pl.multiple_of(blk * 128, 128), 128)], x_sem).start()
        return carry

    lax.fori_loop(0, PAIRS, last_step, 0)
    pltpu.make_async_copy(x, x, x_sem).wait()


def fused_layers(x, positions, norm_attn, norm_mlp, wq, wk, wv, wo, wg, wu, wd, kc, vc):
    half = HD // 2
    freq = (np.float32(ROPE_BASE) ** (-np.arange(half, dtype=np.float32) / np.float32(half))).astype(np.float32)
    freq = jnp.asarray(np.concatenate([freq, freq])[None, :])
    vm = pl.BlockSpec(memory_space=pltpu.VMEM)
    hbm = pl.BlockSpec(memory_space=pl.ANY)
    vmem = pltpu.VMEM
    dma = pltpu.SemaphoreType.DMA
    scratch = [
        vmem((SLOTS, 256, FF), BF16), dma((SLOTS,)),
        vmem((BLKS, ROWS, 128), BF16), dma,
        vmem((2 * LAYERS, 8, DIM), F32),
        vmem((ROWS, HD), F32), vmem((ROWS, HD), F32), vmem((ROWS, HD), F32),
        vmem((ROWS, GROUP * CACHE), F32),
        vmem((ROWS, HD), F32),
        vmem((ROWS, QKV), F32), vmem((QH, ROWS, HD), F32),
        vmem((ROWS, HD), F32), vmem((ROWS, HD), F32),
        vmem((QH, ROWS, HD), F32), vmem((ROWS, QH * HD), BF16),
        vmem((ROWS, FF), F32), vmem((ROWS, FF), F32), vmem((ROWS, FF), BF16),
        vmem((2, ROWS * CACHE, HD), BF16), vmem((2, ROWS * CACHE, HD), BF16), dma((2, 2)),
        vmem((CH, ROWS, 128), F32),
        vmem((CH, ROWS, 128), BF16), vmem((CH, ROWS, 128), BF16),
        vmem((CH, ROWS, 128), BF16), vmem((2, CH, ROWS, 128), BF16),
        dma((CH,)), dma((CH,)), dma((CH,)), dma((2, CH)), dma((CH,)), dma((CH,)),
    ]
    new_rows = jax.ShapeDtypeStruct((LAYERS, ROWS, HD), BF16)
    return pl.pallas_call(
        kernel,
        out_shape=(jax.ShapeDtypeStruct((ROWS, DIM), BF16), new_rows, new_rows),
        in_specs=[hbm, vm, vm, vm, vm] + [hbm] * 9,
        out_specs=(hbm, vm, vm),
        scratch_shapes=scratch,
        compiler_params=pltpu.CompilerParams(collective_id=0, has_side_effects=True, vmem_limit_bytes=67043328),
        name="layers",
    )(x, positions, norm_attn, norm_mlp, freq, wq, wk, wv, wo, wg, wu, wd, kc, vc)


def solution(mesh):
    def local_step(hidden_in, positions, norm_attn, norm_mlp, w_query, w_key, w_value, w_out, w_gate, w_up, w_down, key_cache, value_cache):
        flat = (LAYERS, ROWS * CACHE, HD)
        hidden, k_new, v_new = fused_layers(
            hidden_in, positions[None, :], norm_attn, norm_mlp, w_query, w_key, w_value, w_out, w_gate, w_up, w_down,
            key_cache.reshape(flat), value_cache.reshape(flat))
        write_row = (jnp.arange(CACHE)[None, :] == positions[:, None])[None, :, :, None, None]
        key_out = jnp.where(write_row, k_new[:, :, None, None, :], key_cache)
        value_out = jnp.where(write_row, v_new[:, :, None, None, :], value_cache)
        return hidden, key_out, value_out

    row_spec = P("data", None)
    col_spec = P(None, None, "model")
    split_spec = P(None, "model", None)
    cache_spec = P(None, "data", None, "model", None)
    in_specs = (row_spec, P("data"), P(None, None), P(None, None), col_spec, col_spec, col_spec, split_spec, col_spec, col_spec, split_spec, cache_spec, cache_spec)
    out_specs = (row_spec, cache_spec, cache_spec)
    return jax.shard_map(local_step, mesh=mesh, in_specs=in_specs, out_specs=out_specs, check_vma=False)
```

time: 413 us -> 143 us (0.35); the launches traced: 408 us -> 143 us
  waiting for transfers between devices: 180 us -> 0 us
  matrix products: 175 us -> 0 us
  Pallas kernels: 0 us -> 135 us
  other arithmetic: 33.3 us -> 6.47 us
  between operations: 15.1 us -> 0.65 us
    psum x6 -> x0, waiting for transfers between devices: 180 us -> none  [the longest x3 91.9 us: local_step(): residual = add_residual(residual, lax.psum(attn_part, 'model'))]
    dot_general x21 -> x0, matrix products: 164 us -> none  [the longest x3 75.9 us: local_step(): jnp.dot(act_val, w_down[layer], preferred_element_type=jnp.float32)]
    pallas_call x0 -> x1, Pallas kernels: none -> 135 us  [fused_layers(): pl.pallas_call(kernel, out_shape=(jax.ShapeDtypeStruct((ROWS, DIM), BF16)...]
    sub x3 -> x0, matrix products: 10.9 us -> none  [attention(): attn_prob = jax.nn.softmax(scores, axis=-1).astype(jnp.bfloat16)]
    reduce_sum x6 -> x0, other arithmetic: 10.5 us -> none  [rms_norm(): jnp.mean(vals_f * vals_f, axis=-1, keepdims=True) + NORM_EPS]
    another operation x4 -> x0, other arithmetic: 5.2 us -> none  [the longest x1 3.37 us: local_step(): return (residual, jnp.stack(key_list), jnp.stack(value_list))]
    select_n x2 -> x1, other arithmetic: 8.41 us -> 5.12 us  [local_step(): value_out = jnp.where(write_row, v_new[:, :, None, None, :], value_cache)]
  transfers between devices with their start and end apart: 6 -> 0, of which waited for: 6 -> 0; matrix products, arithmetic and copies ran while one was open for 4% -> 0% of each run, Pallas kernels for 0% -> 0%
where the time goes in v1:
time: 143 us
  Pallas kernels  135 us (94%)
  other arithmetic  6.47 us (5%)
    pallas_call x1, Pallas kernels, fused_layers(): pl.pallas_call(kernel, out_shape=(jax.ShapeDtypeStruct((ROWS, DIM), BF16)...  135 us
    select_n x1, other arithmetic, local_step(): value_out = jnp.where(write_row, v_new[:, :, None, None, :], value_cache)  5.12 us

profile of v1, /device:TPU:0, one launch (start us, length us, event | category | flops | bytes accessed | tf_op | source)
XLA Modules:
  0.0 143.3 jit_solution(16575417260840693292)
XLA Ops:
  0.6 1.3 iota_compare_fusion
  2.0 135.3 %layers.1 = (bf16[128,3584]{1,0:T(8,128)(2,1)}, bf16[3,128,128]{2,1,0:T(8,128)(2,1)}, bf16[3,128,128]{2,1,0:T(8,128)(2,1)}) custom-call(bf16[128,3584]{1,0:T(8,128)(2,1)} %x_hbm.1, s32[1,128]{1,0:T(1,128)} %bitcast.5, bf16[3,3584]{1,0:T(4,128)(2,1)} %na_ref.1, bf16[3,3584]{1,0:T(4,128)(2,1)} %nm_ref.1, f32[1,128]{1,0:T(1,128)} %constant.2.clone.freq_ref, ...), custom_call_target="tpu_custom_call" | custom-call | tf_op jit(solution)/shard_map/layers/pallas_call | solution.py:444
  137.2 0.0 copy-start
  137.2 5.1 %broadcast_select_fusion = (bf16[3,128,32,1,128]{4,2,3,1,0:T(8,128)(2,1)}, bf16[3,128,32,1,128]{4,2,3,1,0:T(8,128)(2,1)}) fusion(bf16[3,128,32,1,128]{4,2,3,1,0:T(8,128)(2,1)} %param.26, pred[128,32]{1,0:T(8,128)(4,1)} %iota_compare_fusion, bf16[3,128,128]{2,1,0:T(8,128)(2,1)} %get-tuple-element.8, bf16[3,128,32,1,128]{4,2,3,1,0:T(8,128)(2,1)} %param.25, ...), kind=kLoop, calls=%fused_computation | loop fusion | flops 3145728 | bytes 12783616 | tf_op jit(solution)/shard_map/jit(_where)/select_n | solution.py:463
  142.4 0.0 copy-done
  142.4 0.9 copy.18
Async XLA Ops:
  137.2 5.1 %copy-start = (bf16[128,3584]{1,0:T(8,128)(2,1)S(1)}, bf16[128,3584]{1,0:T(8,128)(2,1)}, u32[]{:S(2)}) copy-start(bf16[128,3584]{1,0:T(8,128)(2,1)} %get-tuple-element.14) | copy-start | bytes 2752516

commit v2 on v1

v2 whole, which is shorter than its diff:
```python
import functools

import jax
import jax.numpy as jnp
import numpy as np
from jax import lax
from jax.experimental import pallas as pl
from jax.experimental.pallas import tpu as pltpu
from jax.sharding import PartitionSpec as P

NORM_EPS = 1e-6
ROPE_BASE = 10000.0
MESH = pl.DeviceIdType.MESH
F32 = jnp.float32
BF16 = jnp.bfloat16

LAYERS = 3
ROWS = 128
DIM = 3584
HD = 128
QH = 7
CACHE = 32
FF = 4736
BLKS = DIM // 128
PAIRS = DIM // 512
QKV = (QH + 2) * HD
PER_LAYER = 2 + 2 + 2 * PAIRS + PAIRS
SLOTS = 8
DOWN = 2.0 ** -32
UP = 2.0 ** 32
GROUP = 8
GROUPS = ROWS // GROUP
QROWS = (QH + 1) * GROUP
KEYS = GROUP * CACHE


def kernel(x_hbm, pos_ref, na_ref, nm_ref, freq_ref, wq, wk, wv, wo, wg, wu, wd, kc_hbm, vc_hbm,
           out_hbm, kn_out, vn_out, mask_out,
           ring, ring_sem, x, x_sem, gn, posb, cos_t, sin_t, vis, ss, qkv, qs, kn, vn, sc, pr, at, ab, acc_g, acc_u, act,
           kbuf, vbuf, kv_sem, own, a_send, a_recv, b_send, b_recv, a_ss, a_rs, b_ss, b_rs, c_ss, c_rs):
    me = lax.axis_index("model")
    core = lax.rem(me, 2)
    partner = me + 1 - 2 * core
    peer = lax.rem(me + 2, 4)

    def slot_of(n):
        return lax.rem(n, SLOTS)

    def start(layer, r, src, rows, cols):
        s = slot_of(layer * PER_LAYER + r)
        pltpu.make_async_copy(src, ring.at[s, rows, cols], ring_sem.at[s]).start()

    def issue_qkv(layer, r):
        for t in range(4 if r == 0 else 3):
            rows = slice((4 * r + t) * 512, (4 * r + t + 1) * 512)
            base = t * QKV
            start(layer, r, wq.at[layer, rows, :], slice(None), slice(base, base + QH * HD))
            start(layer, r, wk.at[layer, rows, :], slice(None), slice(base + QH * HD, base + (QH + 1) * HD))
            start(layer, r, wv.at[layer, rows, :], slice(None), slice(base + (QH + 1) * HD, base + QKV))

    def issue_out(layer, r):
        if r == 0:
            start(layer, 2, wo.at[layer, 0:512, :], slice(None), slice(0, DIM))
        else:
            start(layer, 3, wo.at[layer, 512:896, :], slice(0, 384), slice(0, DIM))

    def issue_gu(layer, i, which):
        rows = pl.ds(i * 512 if isinstance(i, int) else pl.multiple_of(i * 512, 512), 512)
        src = wu if which else wg
        start(layer, 4 + 2 * i + which, src.at[layer, rows, :], slice(None), slice(None))

    def issue_down(layer, j):
        off = j * 512 if isinstance(j, int) else pl.multiple_of(j * 512, 512)
        for b in range(9):
            start(layer, 18 + j, wd.at[layer, b * 512:(b + 1) * 512, pl.ds(off, 512)], slice(None), slice(b * 512, (b + 1) * 512))
        for q in range(4):
            cols = pl.ds(off + q * 128 if isinstance(j, int) else pl.multiple_of(off + q * 128, 128), 128)
            start(layer, 18 + j, wd.at[layer, 4608:4736, cols], slice(q * 128, (q + 1) * 128), slice(4608, 4736))

    def wait_slot(n, rows, cols):
        s = slot_of(n)
        pltpu.make_async_copy(wg.at[0, :rows, :cols], ring.at[s, :rows, :cols], ring_sem.at[s]).wait()

    def kv_copies(layer):
        b = lax.rem(layer, 2)
        return (pltpu.make_async_copy(kc_hbm.at[layer], kbuf.at[b], kv_sem.at[0, b]),
                pltpu.make_async_copy(vc_hbm.at[layer], vbuf.at[b], kv_sem.at[1, b]))

    barrier = pltpu.get_barrier_semaphore()
    for other in (partner, peer):
        pl.semaphore_signal(barrier, inc=1, device_id={"model": other}, device_id_type=MESH)

    def load_x(b, carry):
        pltpu.make_async_copy(x_hbm.at[:, pl.ds(pl.multiple_of(b * 128, 128), 128)], x.at[b], x_sem).start()
        return carry

    lax.fori_loop(0, BLKS, load_x, 0)

    issue_qkv(0, 0)
    issue_qkv(0, 1)
    for cp in kv_copies(0):
        cp.start()
    issue_out(0, 0)
    issue_out(0, 1)
    for k in range(4):
        issue_gu(0, k // 2, k % 2)

    for layer in range(LAYERS):
        for which, ref in enumerate((na_ref, nm_ref)):
            row = ref[layer:layer + 1, :].astype(F32) * DOWN
            gn[2 * layer + which] = jnp.broadcast_to(row, (8, DIM))
    pos_row = jnp.broadcast_to(pos_ref[...].astype(F32), (ROWS, ROWS))
    ri = lax.broadcasted_iota(jnp.int32, (ROWS, ROWS), 0)
    ci = lax.broadcasted_iota(jnp.int32, (ROWS, ROWS), 1)
    pos_col = jnp.sum(jnp.where(ri == ci, pos_row, 0.0), axis=1, keepdims=True)
    pos_b = jnp.broadcast_to(pos_col, (ROWS, HD))
    posb[...] = pos_b
    angle = pos_b * freq_ref[...]
    cos_t[...] = jnp.cos(angle)
    sin_v = jnp.sin(angle)
    sin_t[...] = jnp.where(ci < HD // 2, -sin_v, sin_v)
    r2 = lax.broadcasted_iota(jnp.int32, (ROWS, GROUP * CACHE), 0)
    c2 = lax.broadcasted_iota(jnp.int32, (ROWS, GROUP * CACHE), 1)
    mine = (c2 // CACHE) == lax.rem(r2, GROUP)
    seen = lax.rem(c2, CACHE).astype(F32) <= jnp.broadcast_to(pos_col, (ROWS, GROUP * CACHE))
    vis[...] = jnp.where(mine & seen, 1.0, 0.0)
    cs = lax.broadcasted_iota(jnp.int32, (ROWS, CACHE), 1).astype(F32)
    mask_out[...] = jnp.where(cs == jnp.broadcast_to(pos_col, (ROWS, CACHE)), 1.0, 0.0)

    pltpu.make_async_copy(x, x, x_sem).wait()
    pl.semaphore_wait(barrier, 2)

    def a_copy(j):
        return pltpu.make_async_remote_copy(a_send.at[j], a_recv.at[j], a_ss.at[j], a_rs.at[j],
                                            device_id={"model": partner}, device_id_type=MESH)

    def b_copy(p, j):
        return pltpu.make_async_remote_copy(b_send.at[j], b_recv.at[p, j], b_ss.at[j], b_rs.at[p, j],
                                            device_id={"model": peer}, device_id_type=MESH)

    def c_copy(j, half):
        blk = pl.ds(4 * j + 2 * half, 2)
        return pltpu.make_async_remote_copy(x.at[blk], x.at[blk], c_ss.at[j], c_rs.at[j],
                                            device_id={"model": partner}, device_id_type=MESH)

    def stage_a(j, part):
        first = core == 0
        for t in range(2):
            lo, hi = part[:, t * 128:(t + 1) * 128], part[:, (t + 2) * 128:(t + 3) * 128]
            own[j, t] = jnp.where(first, lo, hi)
            a_send[j, t] = jnp.where(first, hi, lo).astype(BF16)
        a_copy(j).start()

    def stage_b(p, j):
        a_copy(j).wait_recv()
        b_send[j] = (own[j] + a_recv[j].astype(F32)).astype(BF16)
        b_copy(p, j).start()

    def stage_c(p, j):
        b_copy(p, j).wait_recv()
        total = b_send[j].astype(F32) + b_recv[p, j].astype(F32)
        blk = pl.ds(4 * j + 2 * core, 2)
        x[blk] = (x[blk].astype(F32) + total).astype(BF16)
        c_copy(j, core).start()
        a_copy(j).wait_send()
        b_copy(p, j).wait_send()

    def stage_d(j):
        c_copy(j, 1 - core).wait_recv()
        c_copy(j, core).wait_send()

    def take(row, i):
        outs = []
        sq = ss[...]
        for b in range(4):
            blk = x[4 * i + b].astype(F32)
            sq = sq + blk * blk
            off = i * 512 + b * 128 if isinstance(i, int) else pl.multiple_of(i * 512 + b * 128, 128)
            outs.append((blk * gn[row, 0:1, pl.ds(off, 128)]).astype(BF16))
        ss[...] = sq
        return jnp.concatenate(outs, axis=1)

    def row_scale():
        mean = jnp.sum(ss[...], axis=1, keepdims=True) * (1.0 / DIM)
        return lax.rsqrt(mean + NORM_EPS) * UP

    def dot(a, b):
        return jnp.dot(a, b, preferred_element_type=F32)

    def tiles(width, step):
        return [(n, min(step, width - n)) for n in range(0, width, step)]

    def layer_body(layer, carry):
        base = layer * PER_LAYER
        ss[...] = jnp.zeros_like(ss)
        qkv[...] = jnp.zeros_like(qkv)

        @pl.when(layer > 0)
        def _():
            stage_c(1, 0)

        def qkv_step(i, carry):
            @pl.when((layer > 0) & (i + 1 < PAIRS))
            def _():
                stage_c(1, i + 1)

            @pl.when(layer > 0)
            def _():
                stage_d(i)

            h = take(2 * layer, i)
            s = slot_of(base + i // 4)
            first = lax.rem(i, 4) * QKV
            for c0, w in tiles(QKV, 512):
                qkv[:, c0:c0 + w] += dot(h, ring[s, :, pl.ds(pl.multiple_of(first + c0, 128), w)])
            return carry

        wait_slot(base, 512, 4 * QKV)
        lax.fori_loop(0, 4, qkv_step, 0)
        issue_gu(layer, 2, 0)
        wait_slot(base + 1, 512, 3 * QKV)
        lax.fori_loop(4, PAIRS, qkv_step, 0)
        issue_gu(layer, 2, 1)

        scale = row_scale()
        cos_v, sin_v = cos_t[...], sin_t[...]

        def head(idx):
            return (qkv[:, idx * HD:(idx + 1) * HD] * scale).astype(BF16)

        def rotate(v):
            v = v.astype(F32)
            return (v * cos_v + pltpu.roll(v, HD // 2, axis=1) * sin_v).astype(BF16)

        for h in range(QH):
            qs[h] = rotate(head(h)).astype(F32)
        k_new = rotate(head(QH))
        v_new = head(QH + 1)
        kn[...] = k_new.astype(F32)
        vn[...] = v_new.astype(F32)
        kn_out[layer] = k_new
        vn_out[layer] = v_new
        for cp in kv_copies(layer):
            cp.wait()
        buf = lax.rem(layer, 2)
        srow = lax.rem(lax.broadcasted_iota(jnp.int32, (GROUP * CACHE, HD), 0), CACHE).astype(F32)

        def spread(v):
            return jnp.broadcast_to(v[:, None, :], (GROUP, CACHE, HD)).reshape(GROUP * CACHE, HD)

        span = [slice(g * GROUP, (g + 1) * GROUP) for g in range(GROUPS)]
        cspan = [slice(g * KEYS, (g + 1) * KEYS) for g in range(GROUPS)]
        for g in range(GROUPS):
            here = srow == spread(posb[span[g], :])
            kbuf[buf, cspan[g], :] = jnp.where(here, spread(kn[span[g], :]), kbuf[buf, cspan[g], :].astype(F32)).astype(BF16)
            vbuf[buf, cspan[g], :] = jnp.where(here, spread(vn[span[g], :]), vbuf[buf, cspan[g], :].astype(F32)).astype(BF16)
        for g in range(GROUPS):
            q = jnp.concatenate([qs[h, span[g], :] for h in range(QH)] + [qs[0, span[g], :]], axis=0).astype(BF16)
            sc[g] = lax.dot_general(q, kbuf[buf, cspan[g], :], (((1,), (1,)), ((), ())), preferred_element_type=F32)
        for g in range(GROUPS):
            raw = (sc[g] * (HD ** -0.5)).reshape(QH + 1, GROUP, KEYS)
            raw = jnp.where((vis[span[g], :] > 0.5)[None], raw, -1e30)
            e = jnp.exp(raw - jnp.max(raw, axis=-1, keepdims=True))
            prob = e * (1.0 / jnp.sum(e, axis=-1, keepdims=True))
            pr[g] = prob.reshape(QROWS, KEYS).astype(BF16)
        for g in range(GROUPS):
            o = dot(pr[g], vbuf[buf, cspan[g], :])
            for h in range(QH):
                at[h, span[g], :] = o[h * GROUP:(h + 1) * GROUP]

        @pl.when(layer + 1 < LAYERS)
        def _():
            for cp in kv_copies(layer + 1):
                cp.start()

        for h in range(QH):
            ab[:, h * HD:(h + 1) * HD] = at[h].astype(BF16)

        wait_slot(base + 2, 512, DIM)
        wait_slot(base + 3, 384, DIM)
        for j in range(PAIRS):
            cols = slice(j * 512, (j + 1) * 512)
            part = dot(ab[:, :512], ring[slot_of(base + 2), :, cols]) + dot(ab[:, 512:], ring[slot_of(base + 3), :384, cols])
            stage_a(j, part)
            if j >= 3:
                stage_b(0, j - 3)
        issue_gu(layer, 3, 0)
        issue_gu(layer, 3, 1)
        for j in range(PAIRS - 3, PAIRS):
            stage_b(0, j)

        ss[...] = jnp.zeros_like(ss)
        stage_c(0, 0)

        def gu_step(i, issue, first=False, last=False):
            if not last:
                stage_c(0, i + 1)
            stage_d(i)
            h = take(2 * layer + 1, i)
            n = base + 4 + 2 * i
            for k, acc in ((0, acc_g), (1, acc_u)):
                wait_slot(n + k, 512, FF)
                s = slot_of(n + k)
                for c0, w in tiles(FF, 512):
                    part = dot(h, ring[s, :, c0:c0 + w])
                    if first:
                        acc[:, c0:c0 + w] = part
                    else:
                        acc[:, c0:c0 + w] += part
                issue(k)

        gu_step(0, lambda k: issue_gu(layer, 4, k), first=True)

        def gu_low(i, carry):
            gu_step(i, lambda k: issue_gu(layer, i + 4, k))
            return carry

        def gu_high(i, carry):
            gu_step(i, lambda k: issue_down(layer, 2 * (i - 3) + k))
            return carry

        lax.fori_loop(1, 3, gu_low, 0)
        lax.fori_loop(3, 6, gu_high, 0)

        def issue_last(k):
            if k == 0:
                issue_down(layer, 6)
            else:
                @pl.when(layer + 1 < LAYERS)
                def _():
                    issue_qkv(layer + 1, 0)

        gu_step(6, issue_last, last=True)
        scale2 = row_scale()
        for c0, w in tiles(FF, 512):
            gate = acc_g[:, c0:c0 + w] * scale2
            up = acc_u[:, c0:c0 + w] * scale2
            act[:, c0:c0 + w] = (gate * jax.nn.sigmoid(gate) * up).astype(BF16)

        def down_step(j, issue, lead):
            n = base + 18 + j
            s = slot_of(n)
            wait_slot(n, 512, FF)
            part = dot(act[:, :512], ring[s, :, :512])
            for b in range(1, 9):
                part = part + dot(act[:, b * 512:(b + 1) * 512], ring[s, :, b * 512:(b + 1) * 512])
            last = jnp.concatenate([ring[s, q * 128:(q + 1) * 128, 4608:4736] for q in range(4)], axis=1)
            part = part + dot(act[:, 4608:4736], last)
            stage_a(j, part)

            @pl.when(layer + 1 < LAYERS)
            def _():
                issue()

            if lead:
                stage_b(1, j - 1)

        down_step(0, lambda: issue_qkv(layer + 1, 1), False)
        down_step(1, lambda: issue_out(layer + 1, 0), True)
        down_step(2, lambda: issue_out(layer + 1, 1), True)

        def down_even(t, carry):
            down_step(3 + 2 * t, lambda: issue_gu(layer + 1, t, 0), True)
            down_step(4 + 2 * t, lambda: issue_gu(layer + 1, t, 1), True)
            return carry

        lax.fori_loop(0, 2, down_even, 0)
        stage_b(1, PAIRS - 1)
        return carry

    lax.fori_loop(0, LAYERS, layer_body, 0)

    stage_c(1, 0)

    def last_step(i, carry):
        @pl.when(i + 1 < PAIRS)
        def _():
            stage_c(1, i + 1)

        stage_d(i)
        for b in range(4):
            blk = 4 * i + b
            pltpu.make_async_copy(x.at[blk], out_hbm.at[:, pl.ds(pl.multiple_of(blk * 128, 128), 128)], x_sem).start()
        return carry

    lax.fori_loop(0, PAIRS, last_step, 0)
    pltpu.make_async_copy(x, x, x_sem).wait()


def fused_layers(x, positions, norm_attn, norm_mlp, wq, wk, wv, wo, wg, wu, wd, kc, vc):
    half = HD // 2
    freq = (np.float32(ROPE_BASE) ** (-np.arange(half, dtype=np.float32) / np.float32(half))).astype(np.float32)
    freq = jnp.asarray(np.concatenate([freq, freq])[None, :])
    vm = pl.BlockSpec(memory_space=pltpu.VMEM)
    hbm = pl.BlockSpec(memory_space=pl.ANY)
    vmem = pltpu.VMEM
    dma = pltpu.SemaphoreType.DMA
    scratch = [
        vmem((SLOTS, 512, FF), BF16), dma((SLOTS,)),
        vmem((BLKS, ROWS, 128), BF16), dma,
        vmem((2 * LAYERS, 8, DIM), F32),
        vmem((ROWS, HD), F32), vmem((ROWS, HD), F32), vmem((ROWS, HD), F32),
        vmem((ROWS, GROUP * CACHE), F32),
        vmem((ROWS, HD), F32),
        vmem((ROWS, QKV), F32), vmem((QH, ROWS, HD), F32),
        vmem((ROWS, HD), F32), vmem((ROWS, HD), F32),
        vmem((GROUPS, QROWS, KEYS), F32), vmem((GROUPS, QROWS, KEYS), BF16),
        vmem((QH, ROWS, HD), F32), vmem((ROWS, QH * HD), BF16),
        vmem((ROWS, FF), F32), vmem((ROWS, FF), F32), vmem((ROWS, FF), BF16),
        vmem((2, ROWS * CACHE, HD), BF16), vmem((2, ROWS * CACHE, HD), BF16), dma((2, 2)),
        vmem((PAIRS, 2, ROWS, 128), F32),
        vmem((PAIRS, 2, ROWS, 128), BF16), vmem((PAIRS, 2, ROWS, 128), BF16),
        vmem((PAIRS, 2, ROWS, 128), BF16), vmem((2, PAIRS, 2, ROWS, 128), BF16),
        dma((PAIRS,)), dma((PAIRS,)), dma((PAIRS,)), dma((2, PAIRS)), dma((PAIRS,)), dma((PAIRS,)),
    ]
    new_rows = jax.ShapeDtypeStruct((LAYERS, ROWS, HD), BF16)
    return pl.pallas_call(
        kernel,
        out_shape=(jax.ShapeDtypeStruct((ROWS, DIM), BF16), new_rows, new_rows, jax.ShapeDtypeStruct((ROWS, CACHE), F32)),
        in_specs=[hbm, vm, vm, vm, vm] + [hbm] * 9,
        out_specs=(hbm, vm, vm, vm),
        scratch_shapes=scratch,
        compiler_params=pltpu.CompilerParams(collective_id=0, has_side_effects=True, vmem_limit_bytes=67043328),
        name="layers",
    )(x, positions, norm_attn, norm_mlp, freq, wq, wk, wv, wo, wg, wu, wd, kc, vc)


def solution(mesh):
    def local_step(hidden_in, positions, norm_attn, norm_mlp, w_query, w_key, w_value, w_out, w_gate, w_up, w_down, key_cache, value_cache):
        flat = (LAYERS, ROWS * CACHE, HD)
        hidden, k_new, v_new, mask = fused_layers(
            hidden_in, positions[None, :], norm_attn, norm_mlp, w_query, w_key, w_value, w_out, w_gate, w_up, w_down,
            key_cache.reshape(flat), value_cache.reshape(flat))
        write_row = (mask > 0.5)[None, :, :, None, None]
        key_out = jnp.where(write_row, k_new[:, :, None, None, :], key_cache)
        value_out = jnp.where(write_row, v_new[:, :, None, None, :], value_cache)
        return hidden, key_out, value_out

    row_spec = P("data", None)
    col_spec = P(None, None, "model")
    split_spec = P(None, "model", None)
    cache_spec = P(None, "data", None, "model", None)
    in_specs = (row_spec, P("data"), P(None, None), P(None, None), col_spec, col_spec, col_spec, split_spec, col_spec, col_spec, split_spec, cache_spec, cache_spec)
    out_specs = (row_spec, cache_spec, cache_spec)
    return jax.shard_map(local_step, mesh=mesh, in_specs=in_specs, out_specs=out_specs, check_vma=False)
```

time: 143 us -> 130 us (0.909)
  Pallas kernels: 135 us -> 122 us
    pallas_call x1, Pallas kernels: 135 us -> 122 us  [fused_layers(): pl.pallas_call(kernel, out_shape=(jax.ShapeDtypeStruct((ROWS, DIM), BF16)...]
where the time goes in v2:
time: 130 us
  Pallas kernels  122 us (94%)
  other arithmetic  5.96 us (5%)
    pallas_call x1, Pallas kernels, fused_layers(): pl.pallas_call(kernel, out_shape=(jax.ShapeDtypeStruct((ROWS, DIM), BF16)...  122 us
    select_n x1, other arithmetic, local_step(): value_out = jnp.where(write_row, v_new[:, :, None, None, :], value_cache)  5.11 us

profile of v2, /device:TPU:0, one launch (start us, length us, event | category | flops | bytes accessed | tf_op | source)
XLA Modules:
  0.0 129.8 jit_solution(2963724829536755937)
XLA Ops:
  0.6 122.2 %layers.1 = (bf16[128,3584]{1,0:T(8,128)(2,1)}, bf16[3,128,128]{2,1,0:T(8,128)(2,1)}, bf16[3,128,128]{2,1,0:T(8,128)(2,1)}, f32[128,32]{1,0:T(8,128)}) custom-call(bf16[128,3584]{1,0:T(8,128)(2,1)} %x_hbm.1, s32[1,128]{1,0:T(1,128)} %bitcast.5, bf16[3,3584]{1,0:T(4,128)(2,1)} %na_ref.1, bf16[3,3584]{1,0:T(4,128)(2,1)} %nm_ref.1, ...), custom_call_target="tpu_custom_call" | custom-call | tf_op jit(solution)/shard_map/layers/pallas_call | solution.py:417
  122.9 0.9 broadcast_compare_fusion
  123.7 0.0 copy-start
  123.7 5.1 %broadcast_select_fusion = (bf16[3,128,32,1,128]{4,2,3,1,0:T(8,128)(2,1)}, bf16[3,128,32,1,128]{4,2,3,1,0:T(8,128)(2,1)}) fusion(bf16[3,128,32,1,128]{4,2,3,1,0:T(8,128)(2,1)} %param.26, pred[128,32]{1,0:T(8,128)(4,1)S(1)} %broadcast_compare_fusion, bf16[3,128,128]{2,1,0:T(8,128)(2,1)} %get-tuple-element.10, bf16[3,128,32,1,128]{4,2,3,1,0:T(8,128)(2,1)} %param.25, ...), kind=kLoop, calls=%fused_computation | loop fusion | flops 3145728 | bytes 12783616 | tf_op jit(solution)/shard_map/jit(_where)/select_n | solution.py:436
  128.8 0.0 copy-done
  128.8 0.9 copy.18
Async XLA Ops:
  123.7 5.1 %copy-start = (bf16[128,3584]{1,0:T(8,128)(2,1)S(1)}, bf16[128,3584]{1,0:T(8,128)(2,1)}, u32[]{:S(2)}) copy-start(bf16[128,3584]{1,0:T(8,128)(2,1)} %get-tuple-element.16) | copy-start | bytes 2752516

commit v3 on v2

--- a/solution.py
+++ b/solution.py
@@ -25,7 +25,7 @@
 PAIRS = DIM // 512
 QKV = (QH + 2) * HD
 PER_LAYER = 2 + 2 + 2 * PAIRS + PAIRS
-SLOTS = 8
+SLOTS = 10
 DOWN = 2.0 ** -32
 UP = 2.0 ** 32
 GROUP = 8
@@ -36,12 +36,18 @@
 
 def kernel(x_hbm, pos_ref, na_ref, nm_ref, freq_ref, wq, wk, wv, wo, wg, wu, wd, kc_hbm, vc_hbm,
            out_hbm, kn_out, vn_out, mask_out,
-           ring, ring_sem, x, x_sem, gn, posb, cos_t, sin_t, vis, ss, qkv, qs, kn, vn, sc, pr, at, ab, acc_g, acc_u, act,
+           ring, ring_sem, x, x_sem, gn, posb, cos_t, sin_t, vis, ss, kn, vn, ab, acc_g, acc_u, act,
            kbuf, vbuf, kv_sem, own, a_send, a_recv, b_send, b_recv, a_ss, a_rs, b_ss, b_rs, c_ss, c_rs):
     me = lax.axis_index("model")
     core = lax.rem(me, 2)
     partner = me + 1 - 2 * core
     peer = lax.rem(me + 2, 4)
+
+    at = [acc_u.at[:, h * HD:(h + 1) * HD] for h in range(QH)]
+    qs = [acc_u.at[:, (QH + h) * HD:(QH + h + 1) * HD] for h in range(QH)]
+    qkv = acc_u.at[:, 2 * QH * HD:2 * QH * HD + QKV]
+    sc = [acc_g.at[:QROWS, g * KEYS:(g + 1) * KEYS] for g in range(GROUPS)]
+    pr = [act.at[:QROWS, g * KEYS:(g + 1) * KEYS] for g in range(GROUPS)]
 
     def slot_of(n):
         return lax.rem(n, SLOTS)
@@ -82,9 +88,8 @@
         pltpu.make_async_copy(wg.at[0, :rows, :cols], ring.at[s, :rows, :cols], ring_sem.at[s]).wait()
 
     def kv_copies(layer):
-        b = lax.rem(layer, 2)
-        return (pltpu.make_async_copy(kc_hbm.at[layer], kbuf.at[b], kv_sem.at[0, b]),
-                pltpu.make_async_copy(vc_hbm.at[layer], vbuf.at[b], kv_sem.at[1, b]))
+        return (pltpu.make_async_copy(kc_hbm.at[layer], kbuf, kv_sem.at[0]),
+                pltpu.make_async_copy(vc_hbm.at[layer], vbuf, kv_sem.at[1]))
 
     barrier = pltpu.get_barrier_semaphore()
     for other in (partner, peer):
@@ -102,13 +107,14 @@
         cp.start()
     issue_out(0, 0)
     issue_out(0, 1)
-    for k in range(4):
+    for k in range(6):
         issue_gu(0, k // 2, k % 2)
 
     for layer in range(LAYERS):
         for which, ref in enumerate((na_ref, nm_ref)):
             row = ref[layer:layer + 1, :].astype(F32) * DOWN
-            gn[2 * layer + which] = jnp.broadcast_to(row, (8, DIM))
+            for blk in range(BLKS):
+                gn[2 * layer + which, blk // 4, blk % 4:blk % 4 + 1, :] = row[:, blk * 128:(blk + 1) * 128]
     pos_row = jnp.broadcast_to(pos_ref[...].astype(F32), (ROWS, ROWS))
     ri = lax.broadcasted_iota(jnp.int32, (ROWS, ROWS), 0)
     ci = lax.broadcasted_iota(jnp.int32, (ROWS, ROWS), 1)
@@ -172,11 +178,11 @@
     def take(row, i):
         outs = []
         sq = ss[...]
+        gains = gn[row, i]
         for b in range(4):
             blk = x[4 * i + b].astype(F32)
             sq = sq + blk * blk
-            off = i * 512 + b * 128 if isinstance(i, int) else pl.multiple_of(i * 512 + b * 128, 128)
-            outs.append((blk * gn[row, 0:1, pl.ds(off, 128)]).astype(BF16))
+            outs.append((blk * gains[b:b + 1, :]).astype(BF16))
         ss[...] = sq
         return jnp.concatenate(outs, axis=1)
 
@@ -193,7 +199,7 @@
     def layer_body(layer, carry):
         base = layer * PER_LAYER
         ss[...] = jnp.zeros_like(ss)
-        qkv[...] = jnp.zeros_like(qkv)
+        qkv[...] = jnp.zeros((ROWS, QKV), F32)
 
         @pl.when(layer > 0)
         def _():
@@ -217,10 +223,10 @@
 
         wait_slot(base, 512, 4 * QKV)
         lax.fori_loop(0, 4, qkv_step, 0)
-        issue_gu(layer, 2, 0)
+        issue_gu(layer, 3, 0)
         wait_slot(base + 1, 512, 3 * QKV)
         lax.fori_loop(4, PAIRS, qkv_step, 0)
-        issue_gu(layer, 2, 1)
+        issue_gu(layer, 3, 1)
 
         scale = row_scale()
         cos_v, sin_v = cos_t[...], sin_t[...]
@@ -233,7 +239,7 @@
             return (v * cos_v + pltpu.roll(v, HD // 2, axis=1) * sin_v).astype(BF16)
 
         for h in range(QH):
-            qs[h] = rotate(head(h)).astype(F32)
+            qs[h][...] = rotate(head(h)).astype(F32)
         k_new = rotate(head(QH))
         v_new = head(QH + 1)
         kn[...] = k_new.astype(F32)
@@ -242,7 +248,8 @@
         vn_out[layer] = v_new
         for cp in kv_copies(layer):
             cp.wait()
-        buf = lax.rem(layer, 2)
+        wait_slot(base + 2, 512, DIM)
+        wait_slot(base + 3, 384, DIM)
         srow = lax.rem(lax.broadcasted_iota(jnp.int32, (GROUP * CACHE, HD), 0), CACHE).astype(F32)
 
         def spread(v):
@@ -252,21 +259,21 @@
         cspan = [slice(g * KEYS, (g + 1) * KEYS) for g in range(GROUPS)]
         for g in range(GROUPS):
             here = srow == spread(posb[span[g], :])
-            kbuf[buf, cspan[g], :] = jnp.where(here, spread(kn[span[g], :]), kbuf[buf, cspan[g], :].astype(F32)).astype(BF16)
-            vbuf[buf, cspan[g], :] = jnp.where(here, spread(vn[span[g], :]), vbuf[buf, cspan[g], :].astype(F32)).astype(BF16)
+            kbuf[cspan[g], :] = jnp.where(here, spread(kn[span[g], :]), kbuf[cspan[g], :].astype(F32)).astype(BF16)
+            vbuf[cspan[g], :] = jnp.where(here, spread(vn[span[g], :]), vbuf[cspan[g], :].astype(F32)).astype(BF16)
         for g in range(GROUPS):
-            q = jnp.concatenate([qs[h, span[g], :] for h in range(QH)] + [qs[0, span[g], :]], axis=0).astype(BF16)
-            sc[g] = lax.dot_general(q, kbuf[buf, cspan[g], :], (((1,), (1,)), ((), ())), preferred_element_type=F32)
+            q = jnp.concatenate([qs[h][span[g], :] for h in range(QH)] + [qs[0][span[g], :]], axis=0).astype(BF16)
+            sc[g][...] = lax.dot_general(q, kbuf[cspan[g], :], (((1,), (1,)), ((), ())), preferred_element_type=F32)
         for g in range(GROUPS):
-            raw = (sc[g] * (HD ** -0.5)).reshape(QH + 1, GROUP, KEYS)
+            raw = (sc[g][...] * (HD ** -0.5)).reshape(QH + 1, GROUP, KEYS)
             raw = jnp.where((vis[span[g], :] > 0.5)[None], raw, -1e30)
             e = jnp.exp(raw - jnp.max(raw, axis=-1, keepdims=True))
             prob = e * (1.0 / jnp.sum(e, axis=-1, keepdims=True))
-            pr[g] = prob.reshape(QROWS, KEYS).astype(BF16)
+            pr[g][...] = prob.reshape(QROWS, KEYS).astype(BF16)
         for g in range(GROUPS):
-            o = dot(pr[g], vbuf[buf, cspan[g], :])
+            o = dot(pr[g][...], vbuf[cspan[g], :])
             for h in range(QH):
-                at[h, span[g], :] = o[h * GROUP:(h + 1) * GROUP]
+                at[h][span[g], :] = o[h * GROUP:(h + 1) * GROUP]
 
         @pl.when(layer + 1 < LAYERS)
         def _():
@@ -274,18 +281,16 @@
                 cp.start()
 
         for h in range(QH):
-            ab[:, h * HD:(h + 1) * HD] = at[h].astype(BF16)
-
-        wait_slot(base + 2, 512, DIM)
-        wait_slot(base + 3, 384, DIM)
+            ab[:, h * HD:(h + 1) * HD] = at[h][...].astype(BF16)
+
         for j in range(PAIRS):
             cols = slice(j * 512, (j + 1) * 512)
             part = dot(ab[:, :512], ring[slot_of(base + 2), :, cols]) + dot(ab[:, 512:], ring[slot_of(base + 3), :384, cols])
             stage_a(j, part)
             if j >= 3:
                 stage_b(0, j - 3)
-        issue_gu(layer, 3, 0)
-        issue_gu(layer, 3, 1)
+        issue_gu(layer, 4, 0)
+        issue_gu(layer, 4, 1)
         for j in range(PAIRS - 3, PAIRS):
             stage_b(0, j)
 
@@ -309,28 +314,21 @@
                         acc[:, c0:c0 + w] += part
                 issue(k)
 
-        gu_step(0, lambda k: issue_gu(layer, 4, k), first=True)
-
-        def gu_low(i, carry):
-            gu_step(i, lambda k: issue_gu(layer, i + 4, k))
+        gu_step(0, lambda k: issue_gu(layer, 5, k), first=True)
+        gu_step(1, lambda k: issue_gu(layer, 6, k))
+
+        def gu_mid(i, carry):
+            gu_step(i, lambda k: issue_down(layer, 2 * (i - 2) + k))
             return carry
 
-        def gu_high(i, carry):
-            gu_step(i, lambda k: issue_down(layer, 2 * (i - 3) + k))
-            return carry
-
-        lax.fori_loop(1, 3, gu_low, 0)
-        lax.fori_loop(3, 6, gu_high, 0)
-
-        def issue_last(k):
-            if k == 0:
-                issue_down(layer, 6)
-            else:
-                @pl.when(layer + 1 < LAYERS)
-                def _():
-                    issue_qkv(layer + 1, 0)
-
-        gu_step(6, issue_last, last=True)
+        lax.fori_loop(2, 5, gu_mid, 0)
+
+        def more(fn):
+            pl.when(layer + 1 < LAYERS)(fn)
+
+        gu_step(5, lambda k: more(lambda: issue_qkv(layer + 1, 0)) if k else issue_down(layer, 6))
+        gu_step(6, lambda k: more(lambda: issue_out(layer + 1, 0)) if k else more(lambda: issue_qkv(layer + 1, 1)), last=True)
+        wait_slot(base + 18, 512, FF)
         scale2 = row_scale()
         for c0, w in tiles(FF, 512):
             gate = acc_g[:, c0:c0 + w] * scale2
@@ -340,7 +338,8 @@
         def down_step(j, issue, lead):
             n = base + 18 + j
             s = slot_of(n)
-            wait_slot(n, 512, FF)
+            if lead:
+                wait_slot(n, 512, FF)
             part = dot(act[:, :512], ring[s, :, :512])
             for b in range(1, 9):
                 part = part + dot(act[:, b * 512:(b + 1) * 512], ring[s, :, b * 512:(b + 1) * 512])
@@ -355,16 +354,14 @@
             if lead:
                 stage_b(1, j - 1)
 
-        down_step(0, lambda: issue_qkv(layer + 1, 1), False)
-        down_step(1, lambda: issue_out(layer + 1, 0), True)
-        down_step(2, lambda: issue_out(layer + 1, 1), True)
-
-        def down_even(t, carry):
-            down_step(3 + 2 * t, lambda: issue_gu(layer + 1, t, 0), True)
-            down_step(4 + 2 * t, lambda: issue_gu(layer + 1, t, 1), True)
+        down_step(0, lambda: issue_out(layer + 1, 1), False)
+
+        def down_pair(t, carry):
+            down_step(1 + 2 * t, lambda: issue_gu(layer + 1, t, 0), True)
+            down_step(2 + 2 * t, lambda: issue_gu(layer + 1, t, 1), True)
             return carry
 
-        lax.fori_loop(0, 2, down_even, 0)
+        lax.fori_loop(0, 3, down_pair, 0)
         stage_b(1, PAIRS - 1)
         return carry
 
@@ -398,16 +395,13 @@
     scratch = [
         vmem((SLOTS, 512, FF), BF16), dma((SLOTS,)),
         vmem((BLKS, ROWS, 128), BF16), dma,
-        vmem((2 * LAYERS, 8, DIM), F32),
+        vmem((2 * LAYERS, PAIRS, 8, 128), F32),
         vmem((ROWS, HD), F32), vmem((ROWS, HD), F32), vmem((ROWS, HD), F32),
         vmem((ROWS, GROUP * CACHE), F32),
         vmem((ROWS, HD), F32),
-        vmem((ROWS, QKV), F32), vmem((QH, ROWS, HD), F32),
-        vmem((ROWS, HD), F32), vmem((ROWS, HD), F32),
-        vmem((GROUPS, QROWS, KEYS), F32), vmem((GROUPS, QROWS, KEYS), BF16),
-        vmem((QH, ROWS, HD), F32), vmem((ROWS, QH * HD), BF16),
+        vmem((ROWS, HD), F32), vmem((ROWS, HD), F32), vmem((ROWS, QH * HD), BF16),
         vmem((ROWS, FF), F32), vmem((ROWS, FF), F32), vmem((ROWS, FF), BF16),
-        vmem((2, ROWS * CACHE, HD), BF16), vmem((2, ROWS * CACHE, HD), BF16), dma((2, 2)),
+        vmem((ROWS * CACHE, HD), BF16), vmem((ROWS * CACHE, HD), BF16), dma((2,)),
         vmem((PAIRS, 2, ROWS, 128), F32),
         vmem((PAIRS, 2, ROWS, 128), BF16), vmem((PAIRS, 2, ROWS, 128), BF16),
         vmem((PAIRS, 2, ROWS, 128), BF16), vmem((2, PAIRS, 2, ROWS, 128), BF16),

time: 130 us -> 131 us (level)
  no operation moved by 1% of the time
where the time goes in v3:
time: 131 us
  Pallas kernels  123 us (94%)
  other arithmetic  5.96 us (5%)
    pallas_call x1, Pallas kernels, fused_layers(): pl.pallas_call(kernel, out_shape=(jax.ShapeDtypeStruct((ROWS, DIM), BF16)...  123 us
    select_n x1, other arithmetic, local_step(): value_out = jnp.where(write_row, v_new[:, :, None, None, :], value_cache)  5.11 us

profile of v3, /device:TPU:0, one launch (start us, length us, event | category | flops | bytes accessed | tf_op | source)
XLA Modules:
  0.0 130.9 jit_solution(3863465373688282423)
XLA Ops:
  0.6 123.4 %layers.1 = (bf16[128,3584]{1,0:T(8,128)(2,1)}, bf16[3,128,128]{2,1,0:T(8,128)(2,1)}, bf16[3,128,128]{2,1,0:T(8,128)(2,1)}, f32[128,32]{1,0:T(8,128)}) custom-call(bf16[128,3584]{1,0:T(8,128)(2,1)} %x_hbm.1, s32[1,128]{1,0:T(1,128)} %bitcast.5, bf16[3,3584]{1,0:T(4,128)(2,1)} %na_ref.1, bf16[3,3584]{1,0:T(4,128)(2,1)} %nm_ref.1, ...), custom_call_target="tpu_custom_call" | custom-call | tf_op jit(solution)/shard_map/layers/pallas_call | solution.py:411
  124.0 0.9 broadcast_compare_fusion
  124.9 0.0 copy-start
  124.9 5.1 %broadcast_select_fusion = (bf16[3,128,32,1,128]{4,2,3,1,0:T(8,128)(2,1)}, bf16[3,128,32,1,128]{4,2,3,1,0:T(8,128)(2,1)}) fusion(bf16[3,128,32,1,128]{4,2,3,1,0:T(8,128)(2,1)} %param.26, pred[128,32]{1,0:T(8,128)(4,1)S(1)} %broadcast_compare_fusion, bf16[3,128,128]{2,1,0:T(8,128)(2,1)} %get-tuple-element.10, bf16[3,128,32,1,128]{4,2,3,1,0:T(8,128)(2,1)} %param.25, ...), kind=kLoop, calls=%fused_computation | loop fusion | flops 3145728 | bytes 12783616 | tf_op jit(solution)/shard_map/jit(_where)/select_n | solution.py:430
  130.0 0.0 copy-done
  130.0 0.9 copy.18
Async XLA Ops:
  124.9 5.1 %copy-start = (bf16[128,3584]{1,0:T(8,128)(2,1)S(1)}, bf16[128,3584]{1,0:T(8,128)(2,1)}, u32[]{:S(2)}) copy-start(bf16[128,3584]{1,0:T(8,128)(2,1)} %get-tuple-element.16) | copy-start | bytes 2752516

commit v4 on v3

--- a/solution.py
+++ b/solution.py
@@ -34,8 +34,9 @@
 KEYS = GROUP * CACHE
 
 
-def kernel(x_hbm, pos_ref, na_ref, nm_ref, freq_ref, wq, wk, wv, wo, wg, wu, wd, kc_hbm, vc_hbm,
+def kernel(x_hbm, pos_hbm, na_hbm, nm_hbm, freq_hbm, wq, wk, wv, wo, wg, wu, wd, kc_hbm, vc_hbm,
            out_hbm, kn_out, vn_out, mask_out,
+           pos_ref, na_ref, nm_ref, freq_ref, small_sem, kn16, vn16, mask16, row_sem,
            ring, ring_sem, x, x_sem, gn, posb, cos_t, sin_t, vis, ss, kn, vn, ab, acc_g, acc_u, act,
            kbuf, vbuf, kv_sem, own, a_send, a_recv, b_send, b_recv, a_ss, a_rs, b_ss, b_rs, c_ss, c_rs):
     me = lax.axis_index("model")
@@ -54,7 +55,7 @@
 
     def start(layer, r, src, rows, cols):
         s = slot_of(layer * PER_LAYER + r)
-        pltpu.make_async_copy(src, ring.at[s, rows, cols], ring_sem.at[s]).start()
+        pltpu.make_async_copy(src, ring.at[s, rows, cols], ring_sem.at[s]).start(priority=1)
 
     def issue_qkv(layer, r):
         for t in range(4 if r == 0 else 3):
@@ -95,13 +96,18 @@
     for other in (partner, peer):
         pl.semaphore_signal(barrier, inc=1, device_id={"model": other}, device_id_type=MESH)
 
+    small = [pltpu.make_async_copy(src, dst, small_sem.at[k]) for k, (src, dst) in enumerate((
+        (pos_hbm, pos_ref), (na_hbm, na_ref), (nm_hbm, nm_ref), (freq_hbm, freq_ref)))]
+
     def load_x(b, carry):
         pltpu.make_async_copy(x_hbm.at[:, pl.ds(pl.multiple_of(b * 128, 128), 128)], x.at[b], x_sem).start()
         return carry
 
+
+    issue_qkv(0, 0)
+    for cp in small:
+        cp.start()
     lax.fori_loop(0, BLKS, load_x, 0)
-
-    issue_qkv(0, 0)
     issue_qkv(0, 1)
     for cp in kv_copies(0):
         cp.start()
@@ -110,6 +116,8 @@
     for k in range(6):
         issue_gu(0, k // 2, k % 2)
 
+    for cp in small:
+        cp.wait()
     for layer in range(LAYERS):
         for which, ref in enumerate((na_ref, nm_ref)):
             row = ref[layer:layer + 1, :].astype(F32) * DOWN
@@ -131,7 +139,7 @@
     seen = lax.rem(c2, CACHE).astype(F32) <= jnp.broadcast_to(pos_col, (ROWS, GROUP * CACHE))
     vis[...] = jnp.where(mine & seen, 1.0, 0.0)
     cs = lax.broadcasted_iota(jnp.int32, (ROWS, CACHE), 1).astype(F32)
-    mask_out[...] = jnp.where(cs == jnp.broadcast_to(pos_col, (ROWS, CACHE)), 1.0, 0.0)
+    mask16[...] = jnp.where(cs == jnp.broadcast_to(pos_col, (ROWS, CACHE)), 1.0, 0.0)
 
     pltpu.make_async_copy(x, x, x_sem).wait()
     pl.semaphore_wait(barrier, 2)
@@ -244,8 +252,10 @@
         v_new = head(QH + 1)
         kn[...] = k_new.astype(F32)
         vn[...] = v_new.astype(F32)
-        kn_out[layer] = k_new
-        vn_out[layer] = v_new
+        rows_out = (pltpu.make_async_copy(kn16, kn_out.at[layer], row_sem.at[0]),
+                    pltpu.make_async_copy(vn16, vn_out.at[layer], row_sem.at[1]))
+        kn16[...] = k_new
+        vn16[...] = v_new
         for cp in kv_copies(layer):
             cp.wait()
         wait_slot(base + 2, 512, DIM)
@@ -275,6 +285,9 @@
             for h in range(QH):
                 at[h][span[g], :] = o[h * GROUP:(h + 1) * GROUP]
 
+        for cp in rows_out:
+            cp.start()
+
         @pl.when(layer + 1 < LAYERS)
         def _():
             for cp in kv_copies(layer + 1):
@@ -303,8 +316,9 @@
             stage_d(i)
             h = take(2 * layer + 1, i)
             n = base + 4 + 2 * i
+            wait_slot(n, 512, FF)
+            wait_slot(n + 1, 512, FF)
             for k, acc in ((0, acc_g), (1, acc_u)):
-                wait_slot(n + k, 512, FF)
                 s = slot_of(n + k)
                 for c0, w in tiles(FF, 512):
                     part = dot(h, ring[s, :, c0:c0 + w])
@@ -312,7 +326,8 @@
                         acc[:, c0:c0 + w] = part
                     else:
                         acc[:, c0:c0 + w] += part
-                issue(k)
+            issue(0)
+            issue(1)
 
         gu_step(0, lambda k: issue_gu(layer, 5, k), first=True)
         gu_step(1, lambda k: issue_gu(layer, 6, k))
@@ -363,9 +378,14 @@
 
         lax.fori_loop(0, 3, down_pair, 0)
         stage_b(1, PAIRS - 1)
+        for cp in rows_out:
+            cp.wait()
         return carry
 
+    mask_copy = pltpu.make_async_copy(mask16, mask_out, row_sem.at[2])
+    mask_copy.start()
     lax.fori_loop(0, LAYERS, layer_body, 0)
+    mask_copy.wait()
 
     stage_c(1, 0)
 
@@ -388,11 +408,12 @@
     half = HD // 2
     freq = (np.float32(ROPE_BASE) ** (-np.arange(half, dtype=np.float32) / np.float32(half))).astype(np.float32)
     freq = jnp.asarray(np.concatenate([freq, freq])[None, :])
-    vm = pl.BlockSpec(memory_space=pltpu.VMEM)
     hbm = pl.BlockSpec(memory_space=pl.ANY)
     vmem = pltpu.VMEM
     dma = pltpu.SemaphoreType.DMA
     scratch = [
+        vmem((1, ROWS), jnp.int32), vmem((LAYERS, DIM), BF16), vmem((LAYERS, DIM), BF16), vmem((1, HD), F32), dma((4,)),
+        vmem((ROWS, HD), BF16), vmem((ROWS, HD), BF16), vmem((ROWS, CACHE), F32), dma((3,)),
         vmem((SLOTS, 512, FF), BF16), dma((SLOTS,)),
         vmem((BLKS, ROWS, 128), BF16), dma,
         vmem((2 * LAYERS, PAIRS, 8, 128), F32),
@@ -411,8 +432,8 @@
     return pl.pallas_call(
         kernel,
         out_shape=(jax.ShapeDtypeStruct((ROWS, DIM), BF16), new_rows, new_rows, jax.ShapeDtypeStruct((ROWS, CACHE), F32)),
-        in_specs=[hbm, vm, vm, vm, vm] + [hbm] * 9,
-        out_specs=(hbm, vm, vm, vm),
+        in_specs=[hbm] * 14,
+        out_specs=(hbm,) * 4,
         scratch_shapes=scratch,
         compiler_params=pltpu.CompilerParams(collective_id=0, has_side_effects=True, vmem_limit_bytes=67043328),
         name="layers",

time: 131 us -> 124 us (0.947)
  Pallas kernels: 123 us -> 116 us
    pallas_call x1, Pallas kernels: 123 us -> 116 us  [fused_layers(): pl.pallas_call(kernel, out_shape=(jax.ShapeDtypeStruct((ROWS, DIM), BF16)...]
where the time goes in v4:
time: 124 us
  Pallas kernels  116 us (94%)
  other arithmetic  5.96 us (5%)
    pallas_call x1, Pallas kernels, fused_layers(): pl.pallas_call(kernel, out_shape=(jax.ShapeDtypeStruct((ROWS, DIM), BF16)...  116 us
    select_n x1, other arithmetic, local_step(): value_out = jnp.where(write_row, v_new[:, :, None, None, :], value_cache)  5.11 us

profile of v4, /device:TPU:0, one launch (start us, length us, event | category | flops | bytes accessed | tf_op | source)
XLA Modules:
  0.0 123.8 jit_solution(14535264699517622399)
XLA Ops:
  0.6 116.3 %layers.1 = (bf16[128,3584]{1,0:T(8,128)(2,1)}, bf16[3,128,128]{2,1,0:T(8,128)(2,1)}, bf16[3,128,128]{2,1,0:T(8,128)(2,1)}, f32[128,32]{1,0:T(8,128)}) custom-call(bf16[128,3584]{1,0:T(8,128)(2,1)} %x_hbm.1, s32[1,128]{1,0:T(1,128)} %bitcast.5, bf16[3,3584]{1,0:T(4,128)(2,1)} %na_hbm.1, bf16[3,3584]{1,0:T(4,128)(2,1)} %nm_hbm.1, ...), custom_call_target="tpu_custom_call" | custom-call | tf_op jit(solution)/shard_map/layers/pallas_call | solution.py:432
  116.9 0.9 broadcast_compare_fusion
  117.8 0.0 copy-start
  117.8 5.1 %broadcast_select_fusion = (bf16[3,128,32,1,128]{4,2,3,1,0:T(8,128)(2,1)}, bf16[3,128,32,1,128]{4,2,3,1,0:T(8,128)(2,1)}) fusion(bf16[3,128,32,1,128]{4,2,3,1,0:T(8,128)(2,1)} %param.26, pred[128,32]{1,0:T(8,128)(4,1)S(1)} %broadcast_compare_fusion, bf16[3,128,128]{2,1,0:T(8,128)(2,1)} %get-tuple-element.10, bf16[3,128,32,1,128]{4,2,3,1,0:T(8,128)(2,1)} %param.25, ...), kind=kLoop, calls=%fused_computation | loop fusion | flops 3145728 | bytes 12783616 | tf_op jit(solution)/shard_map/jit(_where)/select_n | solution.py:451
  122.9 0.0 copy-done
  122.9 0.9 copy.18
Async XLA Ops:
  117.8 5.1 %copy-start = (bf16[128,3584]{1,0:T(8,128)(2,1)S(1)}, bf16[128,3584]{1,0:T(8,128)(2,1)}, u32[]{:S(2)}) copy-start(bf16[128,3584]{1,0:T(8,128)(2,1)} %get-tuple-element.16) | copy-start | bytes 2752516

commit v5 on v4

--- a/solution.py
+++ b/solution.py
@@ -35,10 +35,10 @@
 
 
 def kernel(x_hbm, pos_hbm, na_hbm, nm_hbm, freq_hbm, wq, wk, wv, wo, wg, wu, wd, kc_hbm, vc_hbm,
-           out_hbm, kn_out, vn_out, mask_out,
-           pos_ref, na_ref, nm_ref, freq_ref, small_sem, kn16, vn16, mask16, row_sem,
+           out, kc_out, vc_out,
+           pos_ref, na_ref, nm_ref, freq_ref, small_sem,
            ring, ring_sem, x, x_sem, gn, posb, cos_t, sin_t, vis, ss, kn, vn, ab, acc_g, acc_u, act,
-           kbuf, vbuf, kv_sem, own, a_send, a_recv, b_send, b_recv, a_ss, a_rs, b_ss, b_rs, c_ss, c_rs):
+           kv_sem, send, a_recv, b_recv, a_ss, a_rs, b_ss, b_rs, c_ss, c_rs):
     me = lax.axis_index("model")
     core = lax.rem(me, 2)
     partner = me + 1 - 2 * core
@@ -89,8 +89,8 @@
         pltpu.make_async_copy(wg.at[0, :rows, :cols], ring.at[s, :rows, :cols], ring_sem.at[s]).wait()
 
     def kv_copies(layer):
-        return (pltpu.make_async_copy(kc_hbm.at[layer], kbuf, kv_sem.at[0]),
-                pltpu.make_async_copy(vc_hbm.at[layer], vbuf, kv_sem.at[1]))
+        return (pltpu.make_async_copy(kc_hbm.at[layer], kc_out.at[layer], kv_sem.at[0]),
+                pltpu.make_async_copy(vc_hbm.at[layer], vc_out.at[layer], kv_sem.at[1]))
 
     barrier = pltpu.get_barrier_semaphore()
     for other in (partner, peer):
@@ -138,18 +138,16 @@
     mine = (c2 // CACHE) == lax.rem(r2, GROUP)
     seen = lax.rem(c2, CACHE).astype(F32) <= jnp.broadcast_to(pos_col, (ROWS, GROUP * CACHE))
     vis[...] = jnp.where(mine & seen, 1.0, 0.0)
-    cs = lax.broadcasted_iota(jnp.int32, (ROWS, CACHE), 1).astype(F32)
-    mask16[...] = jnp.where(cs == jnp.broadcast_to(pos_col, (ROWS, CACHE)), 1.0, 0.0)
 
     pltpu.make_async_copy(x, x, x_sem).wait()
     pl.semaphore_wait(barrier, 2)
 
     def a_copy(j):
-        return pltpu.make_async_remote_copy(a_send.at[j], a_recv.at[j], a_ss.at[j], a_rs.at[j],
+        return pltpu.make_async_remote_copy(send.at[j], a_recv.at[j], a_ss.at[j], a_rs.at[j],
                                             device_id={"model": partner}, device_id_type=MESH)
 
     def b_copy(p, j):
-        return pltpu.make_async_remote_copy(b_send.at[j], b_recv.at[p, j], b_ss.at[j], b_rs.at[p, j],
+        return pltpu.make_async_remote_copy(send.at[j], b_recv.at[p, j], b_ss.at[j], b_rs.at[p, j],
                                             device_id={"model": peer}, device_id_type=MESH)
 
     def c_copy(j, half):
@@ -157,26 +155,31 @@
         return pltpu.make_async_remote_copy(x.at[blk], x.at[blk], c_ss.at[j], c_rs.at[j],
                                             device_id={"model": partner}, device_id_type=MESH)
 
+    def own_cols(j, t):
+        off = 2 * QH * HD + QKV + (2 * j + t) * 128
+        return pl.ds(off if isinstance(j, int) else pl.multiple_of(off, 128), 128)
+
     def stage_a(j, part):
         first = core == 0
         for t in range(2):
             lo, hi = part[:, t * 128:(t + 1) * 128], part[:, (t + 2) * 128:(t + 3) * 128]
-            own[j, t] = jnp.where(first, lo, hi)
-            a_send[j, t] = jnp.where(first, hi, lo).astype(BF16)
+            acc_u[:, own_cols(j, t)] = jnp.where(first, lo, hi)
+            send[j, t] = jnp.where(first, hi, lo).astype(BF16)
         a_copy(j).start()
 
     def stage_b(p, j):
         a_copy(j).wait_recv()
-        b_send[j] = (own[j] + a_recv[j].astype(F32)).astype(BF16)
+        a_copy(j).wait_send()
+        for t in range(2):
+            send[j, t] = (acc_u[:, own_cols(j, t)] + a_recv[j, t].astype(F32)).astype(BF16)
         b_copy(p, j).start()
 
     def stage_c(p, j):
         b_copy(p, j).wait_recv()
-        total = b_send[j].astype(F32) + b_recv[p, j].astype(F32)
+        total = send[j].astype(F32) + b_recv[p, j].astype(F32)
         blk = pl.ds(4 * j + 2 * core, 2)
         x[blk] = (x[blk].astype(F32) + total).astype(BF16)
         c_copy(j, core).start()
-        a_copy(j).wait_send()
         b_copy(p, j).wait_send()
 
     def stage_d(j):
@@ -252,10 +255,6 @@
         v_new = head(QH + 1)
         kn[...] = k_new.astype(F32)
         vn[...] = v_new.astype(F32)
-        rows_out = (pltpu.make_async_copy(kn16, kn_out.at[layer], row_sem.at[0]),
-                    pltpu.make_async_copy(vn16, vn_out.at[layer], row_sem.at[1]))
-        kn16[...] = k_new
-        vn16[...] = v_new
         for cp in kv_copies(layer):
             cp.wait()
         wait_slot(base + 2, 512, DIM)
@@ -269,11 +268,11 @@
         cspan = [slice(g * KEYS, (g + 1) * KEYS) for g in range(GROUPS)]
         for g in range(GROUPS):
             here = srow == spread(posb[span[g], :])
-            kbuf[cspan[g], :] = jnp.where(here, spread(kn[span[g], :]), kbuf[cspan[g], :].astype(F32)).astype(BF16)
-            vbuf[cspan[g], :] = jnp.where(here, spread(vn[span[g], :]), vbuf[cspan[g], :].astype(F32)).astype(BF16)
+            kc_out[layer, cspan[g], :] = jnp.where(here, spread(kn[span[g], :]), kc_out[layer, cspan[g], :].astype(F32)).astype(BF16)
+            vc_out[layer, cspan[g], :] = jnp.where(here, spread(vn[span[g], :]), vc_out[layer, cspan[g], :].astype(F32)).astype(BF16)
         for g in range(GROUPS):
             q = jnp.concatenate([qs[h][span[g], :] for h in range(QH)] + [qs[0][span[g], :]], axis=0).astype(BF16)
-            sc[g][...] = lax.dot_general(q, kbuf[cspan[g], :], (((1,), (1,)), ((), ())), preferred_element_type=F32)
+            sc[g][...] = lax.dot_general(q, kc_out[layer, cspan[g], :], (((1,), (1,)), ((), ())), preferred_element_type=F32)
         for g in range(GROUPS):
             raw = (sc[g][...] * (HD ** -0.5)).reshape(QH + 1, GROUP, KEYS)
             raw = jnp.where((vis[span[g], :] > 0.5)[None], raw, -1e30)
@@ -281,12 +280,9 @@
             prob = e * (1.0 / jnp.sum(e, axis=-1, keepdims=True))
             pr[g][...] = prob.reshape(QROWS, KEYS).astype(BF16)
         for g in range(GROUPS):
-            o = dot(pr[g][...], vbuf[cspan[g], :])
+            o = dot(pr[g][...], vc_out[layer, cspan[g], :])
             for h in range(QH):
                 at[h][span[g], :] = o[h * GROUP:(h + 1) * GROUP]
-
-        for cp in rows_out:
-            cp.start()
 
         @pl.when(layer + 1 < LAYERS)
         def _():
@@ -378,14 +374,9 @@
 
         lax.fori_loop(0, 3, down_pair, 0)
         stage_b(1, PAIRS - 1)
-        for cp in rows_out:
-            cp.wait()
         return carry
 
-    mask_copy = pltpu.make_async_copy(mask16, mask_out, row_sem.at[2])
-    mask_copy.start()
     lax.fori_loop(0, LAYERS, layer_body, 0)
-    mask_copy.wait()
 
     stage_c(1, 0)
 
@@ -397,11 +388,10 @@
         stage_d(i)
         for b in range(4):
             blk = 4 * i + b
-            pltpu.make_async_copy(x.at[blk], out_hbm.at[:, pl.ds(pl.multiple_of(blk * 128, 128), 128)], x_sem).start()
+            out[:, pl.ds(pl.multiple_of(blk * 128, 128), 128)] = x[blk]
         return carry
 
     lax.fori_loop(0, PAIRS, last_step, 0)
-    pltpu.make_async_copy(x, x, x_sem).wait()
 
 
 def fused_layers(x, positions, norm_attn, norm_mlp, wq, wk, wv, wo, wg, wu, wd, kc, vc):
@@ -413,8 +403,7 @@
     dma = pltpu.SemaphoreType.DMA
     scratch = [
         vmem((1, ROWS), jnp.int32), vmem((LAYERS, DIM), BF16), vmem((LAYERS, DIM), BF16), vmem((1, HD), F32), dma((4,)),
-        vmem((ROWS, HD), BF16), vmem((ROWS, HD), BF16), vmem((ROWS, CACHE), F32), dma((3,)),
-        vmem((SLOTS, 512, FF), BF16), dma((SLOTS,)),
+                vmem((SLOTS, 512, FF), BF16), dma((SLOTS,)),
         vmem((BLKS, ROWS, 128), BF16), dma,
         vmem((2 * LAYERS, PAIRS, 8, 128), F32),
         vmem((ROWS, HD), F32), vmem((ROWS, HD), F32), vmem((ROWS, HD), F32),
@@ -422,20 +411,20 @@
         vmem((ROWS, HD), F32),
         vmem((ROWS, HD), F32), vmem((ROWS, HD), F32), vmem((ROWS, QH * HD), BF16),
         vmem((ROWS, FF), F32), vmem((ROWS, FF), F32), vmem((ROWS, FF), BF16),
-        vmem((ROWS * CACHE, HD), BF16), vmem((ROWS * CACHE, HD), BF16), dma((2,)),
-        vmem((PAIRS, 2, ROWS, 128), F32),
+        dma((2,)),
         vmem((PAIRS, 2, ROWS, 128), BF16), vmem((PAIRS, 2, ROWS, 128), BF16),
-        vmem((PAIRS, 2, ROWS, 128), BF16), vmem((2, PAIRS, 2, ROWS, 128), BF16),
+        vmem((2, PAIRS, 2, ROWS, 128), BF16),
         dma((PAIRS,)), dma((PAIRS,)), dma((PAIRS,)), dma((2, PAIRS)), dma((PAIRS,)), dma((PAIRS,)),
     ]
-    new_rows = jax.ShapeDtypeStruct((LAYERS, ROWS, HD), BF16)
+    caches = vmem((LAYERS, ROWS * CACHE, HD), BF16)
+    vm = pl.BlockSpec(memory_space=pltpu.VMEM)
     return pl.pallas_call(
         kernel,
-        out_shape=(jax.ShapeDtypeStruct((ROWS, DIM), BF16), new_rows, new_rows, jax.ShapeDtypeStruct((ROWS, CACHE), F32)),
+        out_shape=(vmem((ROWS, DIM), BF16), caches, caches),
         in_specs=[hbm] * 14,
-        out_specs=(hbm,) * 4,
+        out_specs=(vm, vm, vm),
         scratch_shapes=scratch,
-        compiler_params=pltpu.CompilerParams(collective_id=0, has_side_effects=True, vmem_limit_bytes=67043328),
+        compiler_params=pltpu.CompilerParams(collective_id=0, has_side_effects=True, vmem_limit_bytes=59800000),
         name="layers",
     )(x, positions, norm_attn, norm_mlp, freq, wq, wk, wv, wo, wg, wu, wd, kc, vc)
 
@@ -443,13 +432,10 @@
 def solution(mesh):
     def local_step(hidden_in, positions, norm_attn, norm_mlp, w_query, w_key, w_value, w_out, w_gate, w_up, w_down, key_cache, value_cache):
         flat = (LAYERS, ROWS * CACHE, HD)
-        hidden, k_new, v_new, mask = fused_layers(
+        hidden, k_out, v_out = fused_layers(
             hidden_in, positions[None, :], norm_attn, norm_mlp, w_query, w_key, w_value, w_out, w_gate, w_up, w_down,
             key_cache.reshape(flat), value_cache.reshape(flat))
-        write_row = (mask > 0.5)[None, :, :, None, None]
-        key_out = jnp.where(write_row, k_new[:, :, None, None, :], key_cache)
-        value_out = jnp.where(write_row, v_new[:, :, None, None, :], value_cache)
-        return hidden, key_out, value_out
+        return hidden, k_out.reshape(key_cache.shape), v_out.reshape(value_cache.shape)
 
     row_spec = P("data", None)
     col_spec = P(None, None, "model")

time: 124 us -> 121 us (0.976)
  other arithmetic: 5.96 us -> 0 us
  local copies, waits for them, and re-layouts: 0.93 us -> 4.25 us
    select_n x1 -> x0, other arithmetic: 5.11 us -> none  [local_step(): value_out = jnp.where(write_row, v_new[:, :, None, None, :], value_cache)]
    unnamed x3, local copies, waits for them, and re-layouts: 0.93 us -> 4.25 us
where the time goes in v5:
time: 121 us
  Pallas kernels  116 us (96%)
  local copies, waits for them, and re-layouts  4.25 us (4%)
    pallas_call x1, Pallas kernels, fused_layers(): pl.pallas_call(kernel, out_shape=(vmem((ROWS, DIM), BF16), caches, caches...  116 us
    unnamed x3, local copies, waits for them, and re-layouts  4.25 us

profile of v5, /device:TPU:0, one launch (start us, length us, event | category | flops | bytes accessed | tf_op | source)
XLA Modules:
  0.0 120.5 jit_solution(10023424376813099089)
XLA Ops:
  0.6 115.6 %layers.1 = (bf16[128,3584]{1,0:T(8,128)(2,1)S(1)}, bf16[3,4096,128]{2,1,0:T(8,128)(2,1)S(1)}, bf16[3,4096,128]{2,1,0:T(8,128)(2,1)S(1)}) custom-call(bf16[128,3584]{1,0:T(8,128)(2,1)} %x_hbm.1, s32[1,128]{1,0:T(1,128)} %bitcast.13, bf16[3,3584]{1,0:T(4,128)(2,1)} %na_hbm.1, bf16[3,3584]{1,0:T(4,128)(2,1)} %nm_hbm.1, f32[1,128]{1,0:T(1,128)} %constant.2.clone.freq_hbm, ...), custom_call_target="tpu_custom_call" | custom-call | tf_op jit(solution)/shard_map/layers/pallas_call | solution.py:421
  116.2 0.9 copy.22
  117.2 1.7 %copy.23 = bf16[3,128,32,1,128]{4,2,3,1,0:T(8,128)(2,1)} copy(bf16[3,128,32,1,128]{4,2,3,1,0:T(8,128)(2,1)S(1)} %bitcast.10) | data formatting | bytes 6291456
  118.8 1.7 %copy.24 = bf16[3,128,32,1,128]{4,2,3,1,0:T(8,128)(2,1)} copy(bf16[3,128,32,1,128]{4,2,3,1,0:T(8,128)(2,1)S(1)} %bitcast.9) | data formatting | bytes 6291456

commit v6 on v5

--- a/solution.py
+++ b/solution.py
@@ -259,17 +259,20 @@
             cp.wait()
         wait_slot(base + 2, 512, DIM)
         wait_slot(base + 3, 384, DIM)
-        srow = lax.rem(lax.broadcasted_iota(jnp.int32, (GROUP * CACHE, HD), 0), CACHE).astype(F32)
+        srow = lax.broadcasted_iota(jnp.int32, (CACHE, HD), 0).astype(F32).astype(BF16)
 
         def spread(v):
             return jnp.broadcast_to(v[:, None, :], (GROUP, CACHE, HD)).reshape(GROUP * CACHE, HD)
 
         span = [slice(g * GROUP, (g + 1) * GROUP) for g in range(GROUPS)]
         cspan = [slice(g * KEYS, (g + 1) * KEYS) for g in range(GROUPS)]
-        for g in range(GROUPS):
-            here = srow == spread(posb[span[g], :])
-            kc_out[layer, cspan[g], :] = jnp.where(here, spread(kn[span[g], :]), kc_out[layer, cspan[g], :].astype(F32)).astype(BF16)
-            vc_out[layer, cspan[g], :] = jnp.where(here, spread(vn[span[g], :]), vc_out[layer, cspan[g], :].astype(F32)).astype(BF16)
+        for t in range(ROWS):
+            trow = slice(t * CACHE, (t + 1) * CACHE)
+            here = srow == jnp.broadcast_to(posb[t:t + 1, :], (CACHE, HD)).astype(BF16)
+            k_row = jnp.broadcast_to(kn[t:t + 1, :], (CACHE, HD)).astype(BF16)
+            v_row = jnp.broadcast_to(vn[t:t + 1, :], (CACHE, HD)).astype(BF16)
+            kc_out[layer, trow, :] = jnp.where(here, k_row, kc_out[layer, trow, :])
+            vc_out[layer, trow, :] = jnp.where(here, v_row, vc_out[layer, trow, :])
         for g in range(GROUPS):
             q = jnp.concatenate([qs[h][span[g], :] for h in range(QH)] + [qs[0][span[g], :]], axis=0).astype(BF16)
             sc[g][...] = lax.dot_general(q, kc_out[layer, cspan[g], :], (((1,), (1,)), ((), ())), preferred_element_type=F32)
@@ -429,12 +432,36 @@
     )(x, positions, norm_attn, norm_mlp, freq, wq, wk, wv, wo, wg, wu, wd, kc, vc)
 
 
+def flush_kernel(x_ref, k_ref, v_ref, x_out, k_out, v_out, sem):
+    pieces = [(x_ref, x_out)]
+    for layer in range(LAYERS):
+        pieces += [(k_ref.at[layer], k_out.at[layer]), (v_ref.at[layer], v_out.at[layer])]
+    copies = [pltpu.make_async_copy(src, dst, sem.at[n]) for n, (src, dst) in enumerate(pieces)]
+    for cp in copies:
+        cp.start()
+    for cp in copies:
+        cp.wait()
+
+
+def write_back(*arrays):
+    return pl.pallas_call(
+        flush_kernel,
+        out_shape=tuple(jax.ShapeDtypeStruct(a.shape, a.dtype) for a in arrays),
+        in_specs=[pl.BlockSpec(memory_space=pltpu.VMEM)] * 3,
+        out_specs=(pl.BlockSpec(memory_space=pl.ANY),) * 3,
+        scratch_shapes=[pltpu.SemaphoreType.DMA((1 + 2 * LAYERS,))],
+        compiler_params=pltpu.CompilerParams(vmem_limit_bytes=16 * 2 ** 20),
+        name="write_back",
+    )(*arrays)
+
+
 def solution(mesh):
     def local_step(hidden_in, positions, norm_attn, norm_mlp, w_query, w_key, w_value, w_out, w_gate, w_up, w_down, key_cache, value_cache):
         flat = (LAYERS, ROWS * CACHE, HD)
         hidden, k_out, v_out = fused_layers(
             hidden_in, positions[None, :], norm_attn, norm_mlp, w_query, w_key, w_value, w_out, w_gate, w_up, w_down,
             key_cache.reshape(flat), value_cache.reshape(flat))
+        hidden, k_out, v_out = write_back(hidden, k_out, v_out)
         return hidden, k_out.reshape(key_cache.shape), v_out.reshape(value_cache.shape)
 
     row_spec = P("data", None)

time: 121 us -> 119 us (0.983)
  local copies, waits for them, and re-layouts: 4.25 us -> 0 us
  Pallas kernels: 116 us -> 118 us
    unnamed x3 -> x0, local copies, waits for them, and re-layouts: 4.25 us -> none
    pallas_call x0 -> x1, Pallas kernels: none -> 3.03 us  [write_back(): pl.pallas_call(flush_kernel, out_shape=tuple((jax.ShapeDtypeStruct(a.shap...]
where the time goes in v6:
time: 119 us
  Pallas kernels  118 us (99%)
    pallas_call x1, Pallas kernels, fused_layers(): pl.pallas_call(kernel, out_shape=(vmem((ROWS, DIM), BF16), caches, caches...  115 us
    pallas_call x1, Pallas kernels, write_back(): pl.pallas_call(flush_kernel, out_shape=tuple((jax.ShapeDtypeStruct(a.shap...  3.03 us

profile of v6, /device:TPU:0, one launch (start us, length us, event | category | flops | bytes accessed | tf_op | source)
XLA Modules:
  0.0 119.0 jit_solution(4503306952649633521)
XLA Ops:
  0.6 115.3 %layers.1 = (bf16[128,3584]{1,0:T(8,128)(2,1)S(1)}, bf16[3,4096,128]{2,1,0:T(8,128)(2,1)S(1)}, bf16[3,4096,128]{2,1,0:T(8,128)(2,1)S(1)}) custom-call(bf16[128,3584]{1,0:T(8,128)(2,1)} %x_hbm.1, s32[1,128]{1,0:T(1,128)} %bitcast.11, bf16[3,3584]{1,0:T(4,128)(2,1)} %na_hbm.1, bf16[3,3584]{1,0:T(4,128)(2,1)} %nm_hbm.1, f32[1,128]{1,0:T(1,128)} %constant.2.clone.freq_hbm, ...), custom_call_target="tpu_custom_call" | custom-call | tf_op jit(solution)/shard_map/layers/pallas_call | solution.py:424
  116.0 3.0 %write_back.1 = (bf16[128,3584]{1,0:T(8,128)(2,1)}, bf16[3,4096,128]{2,1,0:T(8,128)(2,1)}, bf16[3,4096,128]{2,1,0:T(8,128)(2,1)}) custom-call(bf16[128,3584]{1,0:T(8,128)(2,1)S(1)} %get-tuple-element.9.x_ref, bf16[3,4096,128]{2,1,0:T(8,128)(2,1)S(1)} %get-tuple-element.10.k_ref, bf16[3,4096,128]{2,1,0:T(8,128)(2,1)S(1)} %get-tuple-element.11.v_ref), custom_call_target="tpu_custom_call" | custom-call | tf_op jit(solution)/shard_map/write_back/pallas_call | solution.py:447

commit v7 on v6

--- a/solution.py
+++ b/solution.py
@@ -287,11 +287,6 @@
             for h in range(QH):
                 at[h][span[g], :] = o[h * GROUP:(h + 1) * GROUP]
 
-        @pl.when(layer + 1 < LAYERS)
-        def _():
-            for cp in kv_copies(layer + 1):
-                cp.start()
-
         for h in range(QH):
             ab[:, h * HD:(h + 1) * HD] = at[h][...].astype(BF16)
 
@@ -299,11 +294,11 @@
             cols = slice(j * 512, (j + 1) * 512)
             part = dot(ab[:, :512], ring[slot_of(base + 2), :, cols]) + dot(ab[:, 512:], ring[slot_of(base + 3), :384, cols])
             stage_a(j, part)
-            if j >= 3:
-                stage_b(0, j - 3)
+            if j >= 2:
+                stage_b(0, j - 2)
         issue_gu(layer, 4, 0)
         issue_gu(layer, 4, 1)
-        for j in range(PAIRS - 3, PAIRS):
+        for j in range(PAIRS - 2, PAIRS):
             stage_b(0, j)
 
         ss[...] = jnp.zeros_like(ss)
@@ -343,6 +338,11 @@
         gu_step(5, lambda k: more(lambda: issue_qkv(layer + 1, 0)) if k else issue_down(layer, 6))
         gu_step(6, lambda k: more(lambda: issue_out(layer + 1, 0)) if k else more(lambda: issue_qkv(layer + 1, 1)), last=True)
         wait_slot(base + 18, 512, FF)
+        @pl.when(layer + 1 < LAYERS)
+        def _():
+            for cp in kv_copies(layer + 1):
+                cp.start()
+
         scale2 = row_scale()
         for c0, w in tiles(FF, 512):
             gate = acc_g[:, c0:c0 + w] * scale2

time: 119 us -> 119 us (level)
  no operation moved by 1% of the time
where the time goes in v7:
time: 119 us
  Pallas kernels  118 us (99%)
    pallas_call x1, Pallas kernels, fused_layers(): pl.pallas_call(kernel, out_shape=(vmem((ROWS, DIM), BF16), caches, caches...  115 us
    pallas_call x1, Pallas kernels, write_back(): pl.pallas_call(flush_kernel, out_shape=tuple((jax.ShapeDtypeStruct(a.shap...  3.03 us

profile of v7, /device:TPU:0, one launch (start us, length us, event | category | flops | bytes accessed | tf_op | source)
XLA Modules:
  0.0 118.9 jit_solution(4532565208031390535)
XLA Ops:
  0.6 115.2 %layers.1 = (bf16[128,3584]{1,0:T(8,128)(2,1)S(1)}, bf16[3,4096,128]{2,1,0:T(8,128)(2,1)S(1)}, bf16[3,4096,128]{2,1,0:T(8,128)(2,1)S(1)}) custom-call(bf16[128,3584]{1,0:T(8,128)(2,1)} %x_hbm.1, s32[1,128]{1,0:T(1,128)} %bitcast.11, bf16[3,3584]{1,0:T(4,128)(2,1)} %na_hbm.1, bf16[3,3584]{1,0:T(4,128)(2,1)} %nm_hbm.1, f32[1,128]{1,0:T(1,128)} %constant.2.clone.freq_hbm, ...), custom_call_target="tpu_custom_call" | custom-call | tf_op jit(solution)/shard_map/layers/pallas_call | solution.py:424
  115.8 3.0 %write_back.1 = (bf16[128,3584]{1,0:T(8,128)(2,1)}, bf16[3,4096,128]{2,1,0:T(8,128)(2,1)}, bf16[3,4096,128]{2,1,0:T(8,128)(2,1)}) custom-call(bf16[128,3584]{1,0:T(8,128)(2,1)S(1)} %get-tuple-element.9.x_ref, bf16[3,4096,128]{2,1,0:T(8,128)(2,1)S(1)} %get-tuple-element.10.k_ref, bf16[3,4096,128]{2,1,0:T(8,128)(2,1)S(1)} %get-tuple-element.11.v_ref), custom_call_target="tpu_custom_call" | custom-call | tf_op jit(solution)/shard_map/write_back/pallas_call | solution.py:447
